TPU v7x, 128 devices: a whole 4x4x4 slice. The times are simulated.
128 devices in a mesh: dp: 2 (over core), ctx: 64 (over z, y, x).
Axes of the slice: x: 4, y: 4, z: 4, core: 2. Of those that a mesh axis runs over, the one named last changes fastest.
Arguments:
- documents: int32 [32768], P(('dp', 'ctx')), parts along dimension 0, may hold values from 0 to 15, never falling along the last dimension, each value on 1 to 2048 neighbouring positions
- queries: bfloat16 [32768, 4096], P(('dp', 'ctx')), parts along dimension 0, may hold values from -6 to 6
- key_projection_rows: bfloat16 [32768, 512], P(('dp', 'ctx')), parts along dimension 0, may hold values from -6 to 6
- value_projection_rows: bfloat16 [32768, 512], P(('dp', 'ctx')), parts along dimension 0, may hold values from -6 to 6
Outputs:
- attended: bfloat16 [32768, 4096], P(('dp', 'ctx')), parts along dimension 0
There are 2 independent parts, one for each index of `dp`. A program takes and returns all parts, laid end to end along the dimension named above; each array names one. Nothing has to cross between parts.
Inputs may be any that keep to these rules, and one draw needn't show every extreme that they name: `documents`: document numbers never fall along the sequence; every number appears; each document has 1 to 2048 tokens and one has exactly 2048.
All inputs are finite; a program needn't handle non-finite values.
Results may differ from a plain program's by a relative error of at most 0.0074.
Values may be sent and summed in bfloat16 or wider, within the bound.
A program may use at most 192 MiB of HBM per device.

v0:
```python
import functools
import math
import jax
import jax.numpy as jnp
import numpy as np
from jax import lax
from jax.experimental import pallas as pl
from jax.experimental.pallas import tpu as pltpu
from jax.sharding import PartitionSpec as P

HEAD = 128
HEADS = 32
KV_HEADS = 4
GROUP = HEADS // KV_HEADS
ROWS = 256
ITEMS = 9
VALUE_ROWS = 144
AT_ONCE = 4
MOST_AT_ONCE = 3
SCALE = math.log2(math.e) / math.sqrt(HEAD)
LOW = 1e-25
HIGH = 1e37
MASKED = -1e30
MESH = pl.DeviceIdType.MESH
VMEM = pltpu.VMEM


def attend(docs, inverse, q_hbm, k_ref, v_ref, ot_hbm, qt_hbm, wk_hbm, wv_hbm, start_out, bad_out,
           q_buf, q_t, wk, wv, bias, acc, probs, o_t, doc_win, cosine, sine,
           rk, rv, sk, sv, doc_send, doc_recv, q_sem, ot_sem, qt_sem, wk_sem, wv_sem):
    count = lax.axis_size("ctx")
    me = lax.axis_index("ctx")
    x = lax.rem(me, 4)
    row = me - x
    right = row + lax.rem(x + 1, 4)
    left = row + lax.rem(x + 3, 4)
    up = lax.rem(me + 4, count)

    barrier = pltpu.get_barrier_semaphore()
    for other in [lax.rem(me + count - d, count) for d in range(1, 9)] + [left, right]:
        pl.semaphore_signal(barrier, inc=1, device_id={"ctx": other}, device_id_type=MESH)
    q_copy = pltpu.make_async_copy(q_hbm, q_buf, q_sem)
    q_copy.start()

    def value_copy(src, dst, c, target):
        return pltpu.make_async_remote_copy(
            wv.at[src, c, pl.ds(0, HEAD)], wv.at[dst, c, pl.ds(0, HEAD)], sv.at[dst, c], rv.at[dst, c],
            device_id={"ctx": target}, device_id_type=MESH)

    def key_copy(src, dst, c, target):
        return pltpu.make_async_remote_copy(
            wk.at[src, c], wk.at[dst, c], sk.at[dst, c], rk.at[dst, c],
            device_id={"ctx": target}, device_id_type=MESH)

    def doc_copy(d):
        return pltpu.make_async_remote_copy(
            docs, doc_win.at[d - 1], doc_send.at[d - 1], doc_recv.at[d - 1],
            device_id={"ctx": lax.rem(me + d, count)}, device_id_type=MESH)

    def when_sent(condition, copy):
        @pl.when(condition)
        def _():
            copy.start()

    wv[:, :, HEAD:, :] = jnp.ones((ITEMS, KV_HEADS, VALUE_ROWS - HEAD, ROWS), jnp.bfloat16)
    for c in range(KV_HEADS):
        wv[0, c, 0:HEAD] = v_ref[:, c * HEAD:(c + 1) * HEAD].T
    pl.semaphore_wait(barrier, 10)
    for d in range(1, 9):
        doc_copy(d).start()
    for c in range(KV_HEADS):
        value_copy(0, 4, c, up).start()
        when_sent(x < 3, value_copy(0, 1, c, right))
        when_sent(x == 0, value_copy(0, 3, c, left))

    doc_row = docs[...].astype(jnp.float32)
    columns = jnp.transpose(jnp.broadcast_to(doc_row, (ROWS, ROWS)))
    local = jnp.sum((columns < doc_row).astype(jnp.float32), axis=0, keepdims=True)
    first = doc_row[:, 0:1]
    for d in range(1, 9):
        doc_copy(d).wait_recv()
    behind = jnp.zeros((1, ROWS), jnp.float32)
    for d in range(1, 9):
        same = (doc_win[d - 1].astype(jnp.float32) == first).astype(jnp.float32)
        behind = behind + same * jnp.where(d <= me, 1.0, 0.0)
    behind = jnp.sum(behind, axis=1, keepdims=True)
    start = jnp.where(doc_row == first, -behind, local)
    start_out[...] = jnp.broadcast_to(start, (8, ROWS))
    tokens = lax.broadcasted_iota(jnp.int32, (1, ROWS), 1).astype(jnp.float32)
    angles = inverse[...] * (tokens - start)
    cosine[...] = jnp.cos(angles)
    sine[...] = jnp.sin(angles)

    def rotated(matrix):
        wide = matrix.astype(jnp.float32)
        a, b = wide[0:HEAD // 2], wide[HEAD // 2:]
        co, si = cosine[...], sine[...]
        return jnp.concatenate([a * co - b * si, b * co + a * si], axis=0)

    for c in range(KV_HEADS):
        wk[0, c] = rotated(k_ref[:, c * HEAD:(c + 1) * HEAD].T).T.astype(jnp.bfloat16)

    query = lax.broadcasted_iota(jnp.int32, (ROWS, ROWS), 1).astype(jnp.float32)
    key = lax.broadcasted_iota(jnp.int32, (ROWS, ROWS), 0).astype(jnp.float32)
    for d in range(ITEMS):
        at = key - float(ROWS * d)
        bias[d] = jnp.where((at >= start) & (at <= query), 0.0, MASKED)

    for c in range(KV_HEADS):
        key_copy(0, 4, c, up).start()
        when_sent(x < 3, key_copy(0, 1, c, right))
        when_sent(x == 0, key_copy(0, 3, c, left))

    def here(values, keys, c):
        for d in values:
            value_copy(d, d, c, up).wait_recv()
        for d in keys:
            key_copy(d, d, c, up).wait_recv()

    q_copy.wait()

    def step_one(c, _):
        here((4,), (), c)
        when_sent(x == 3, value_copy(4, 1, c, right))
        when_sent(x > 0, value_copy(4, 3, c, left))

        def turn(h, _):
            at = pl.multiple_of(h * HEAD, HEAD)
            q_t[h] = rotated(q_buf[:, pl.ds(at, HEAD)].T).astype(jnp.bfloat16)
            return 0

        lax.fori_loop(c * GROUP, c * GROUP + GROUP, turn, 0)
        return 0

    lax.fori_loop(0, KV_HEADS, step_one, 0)
    qt_copy = pltpu.make_async_copy(q_t, qt_hbm, qt_sem)
    qt_copy.start()
    bad_out[...] = jnp.zeros((8, ROWS), jnp.float32)

    def weigh(items, at):
        for u in range(AT_ONCE):
            h = at + u
            for n, d in enumerate(items):
                scores = lax.dot_general(wk[d, h // GROUP], q_t[h], (((1,), (0,)), ((), ())),
                                         preferred_element_type=jnp.float32)
                probs[u, n] = jnp.exp2(scores * SCALE + bias[d]).astype(jnp.bfloat16)

    def gather(items, at, begin, end):
        for u in range(AT_ONCE):
            h = at + u
            kv = jnp.maximum(h, 0) // GROUP
            total = None
            for n, d in enumerate(items):
                part = lax.dot_general(wv[d, kv], probs[u, n], (((1,), (0,)), ((), ())),
                                       preferred_element_type=jnp.float32)
                total = part if total is None else total + part
            if not begin:
                total = acc[h + AT_ONCE] + total
            if end:
                bottom = total[HEAD:HEAD + 1]
                o_t[h + AT_ONCE] = (total[0:HEAD] * (1.0 / bottom)).astype(jnp.bfloat16)
                fine = (bottom >= LOW) & (bottom <= HIGH)
                fine = fine | (h < 0)
                bad_out[0:1] = jnp.maximum(bad_out[0:1], jnp.where(fine, 0.0, 1.0))
            else:
                acc[h + AT_ONCE] = total

    def out_copy(i):
        return pltpu.make_async_copy(o_t.at[pl.ds(AT_ONCE * (i + 1), AT_ONCE)],
                                     ot_hbm.at[pl.ds(AT_ONCE * i, AT_ONCE)], ot_sem.at[i])

    def group(items, event, begin=False, end=False):
        def outer(c, _):
            event(c)

            def inner(j, _):
                i = 2 * c + j
                if end:
                    @pl.when(i >= 2)
                    def _():
                        out_copy(i - 2).start()
                gather(items, AT_ONCE * (i - 1), begin, end)
                weigh(items, AT_ONCE * i)
                return 0

            lax.fori_loop(0, 2, inner, 0)
            return 0

        lax.fori_loop(0, KV_HEADS, outer, 0)
        if end:
            out_copy(6).start()
        gather(items, HEADS - AT_ONCE, begin, end)

    def event_two(c):
        here((), (4,), c)
        value_copy(4, 8, c, up).start()
        when_sent(x < 3, value_copy(4, 5, c, right))
        when_sent(x == 3, key_copy(4, 1, c, right))
        when_sent(x > 0, key_copy(4, 3, c, left))

    def event_three(c):
        here((1, 8), (3,), c)
        key_copy(3, 7, c, up).start()
        when_sent(x < 3, value_copy(1, 2, c, right))
        when_sent(x == 3, value_copy(8, 5, c, right))
        when_sent(x > 0, value_copy(8, 7, c, left))
        when_sent(x == 0, value_copy(4, 7, c, left))

    def event_four(c):
        here((3, 5, 7), (1,), c)
        key_copy(1, 5, c, up).start()
        when_sent(x < 3, key_copy(1, 2, c, right))
        when_sent(x == 3, value_copy(5, 2, c, right))
        when_sent(x > 0, value_copy(7, 6, c, left))
        when_sent(x == 0, value_copy(3, 6, c, left))

    def event_five(c):
        here((), (5, 7), c)
        key_copy(4, 8, c, up).start()
        when_sent(x == 3, key_copy(5, 2, c, right))
        when_sent(x > 0, key_copy(7, 6, c, left))
        when_sent(x == 0, key_copy(3, 6, c, left))

    def event_six(c):
        here((2, 6), (2, 6, 8), c)

    def kept(refs, out, sems, d):
        return pltpu.make_async_copy(refs.at[d], out.at[d], sems.at[d])

    def keep(*items):
        for d in items:
            kept(wk, wk_hbm, wk_sem, d).start()
            kept(wv, wv_hbm, wv_sem, d).start()

    group((0,), event_two, begin=True)
    keep(0, 4)
    group((4,), event_three)
    group((1, 3), event_four)
    keep(1, 3)
    group((5, 7), event_five)
    keep(5, 7)
    group((2, 6, 8), event_six, end=True)
    keep(2, 6, 8)
    out_copy(7).start()

    for d in range(ITEMS):
        kept(wk, wk_hbm, wk_sem, d).wait()
        kept(wv, wv_hbm, wv_sem, d).wait()
    for i in range(HEADS // AT_ONCE):
        out_copy(i).wait()
    qt_copy.wait()
    for d in range(1, 9):
        doc_copy(d).wait_send()

    def drain(c, _):
        for d in range(1, 9):
            value_copy(d, d, c, up).wait_send()
            key_copy(d, d, c, up).wait_send()
        return 0

    lax.fori_loop(0, KV_HEADS, drain, 0)


def finish(o_t, start, bad, qt_hbm, wk_hbm, wv_hbm, out, q_buf, k_buf, v_buf, sems):
    g = pl.program_id(0)
    fine = jnp.max(bad[...]) < 0.5

    @pl.when(fine)
    def _():
        for u in range(GROUP):
            out[:, u * HEAD:(u + 1) * HEAD] = o_t[u].T

    @pl.when(jnp.logical_not(fine))
    def _():
        copies = [
            pltpu.make_async_copy(qt_hbm.at[pl.ds(GROUP * g, GROUP)], q_buf, sems.at[0]),
            pltpu.make_async_copy(wk_hbm.at[:, g], k_buf, sems.at[1]),
            pltpu.make_async_copy(wv_hbm.at[:, g], v_buf, sems.at[2]),
        ]
        for copy in copies:
            copy.start()
        for copy in copies:
            copy.wait()
        query = lax.broadcasted_iota(jnp.int32, (ROWS, ROWS), 1).astype(jnp.float32)
        key = lax.broadcasted_iota(jnp.int32, (ROWS, ROWS), 0).astype(jnp.float32)
        begin = start[0:1]

        for u in range(GROUP):
            def scores(d):
                at = key - (d * ROWS).astype(jnp.float32)
                found = lax.dot_general(k_buf[d], q_buf[u], (((1,), (0,)), ((), ())),
                                        preferred_element_type=jnp.float32)
                return jnp.where((at >= begin) & (at <= query), found * SCALE, MASKED)

            def highest(d, top):
                return jnp.maximum(top, jnp.max(scores(d), axis=0, keepdims=True))

            top = lax.fori_loop(0, ITEMS, highest, jnp.full((1, ROWS), MASKED, jnp.float32))

            def summed(d, carry):
                bottom, total = carry
                weights = jnp.exp2(scores(d) - top)
                bottom = bottom + jnp.sum(weights, axis=0, keepdims=True)
                part = lax.dot_general(v_buf[d, 0:HEAD], weights.astype(jnp.bfloat16), (((1,), (0,)), ((), ())),
                                       preferred_element_type=jnp.float32)
                return bottom, total + part

            bottom, total = lax.fori_loop(
                0, ITEMS, summed, (jnp.zeros((1, ROWS), jnp.float32), jnp.zeros((HEAD, ROWS), jnp.float32)))
            out[:, u * HEAD:(u + 1) * HEAD] = (total / bottom).astype(jnp.bfloat16).T


def shards(documents, queries, key_projection_rows, value_projection_rows):
    bf, f32 = jnp.bfloat16, jnp.float32
    powers = np.float32(1000000.0) ** (-2.0 * np.arange(HEAD // 2, dtype=np.float32) / HEAD)
    inverse = jnp.asarray(np.broadcast_to(powers[:, None], (HEAD // 2, ROWS)), f32)
    vmem, whole = pl.BlockSpec(memory_space=VMEM), pl.BlockSpec(memory_space=pl.ANY)
    dma = pltpu.SemaphoreType.DMA
    flops = 4 * HEADS * ROWS * ITEMS * ROWS * HEAD
    o_t, q_t, wk, wv, start, bad = pl.pallas_call(
        attend,
        out_shape=[
            jax.ShapeDtypeStruct((HEADS, HEAD, ROWS), bf),
            jax.ShapeDtypeStruct((HEADS, HEAD, ROWS), bf),
            jax.ShapeDtypeStruct((ITEMS, KV_HEADS, ROWS, HEAD), bf),
            jax.ShapeDtypeStruct((ITEMS, KV_HEADS, VALUE_ROWS, ROWS), bf),
            jax.ShapeDtypeStruct((8, ROWS), f32),
            jax.ShapeDtypeStruct((8, ROWS), f32),
        ],
        in_specs=[vmem, vmem, whole, vmem, vmem],
        out_specs=[whole] * 4 + [vmem] * 2,
        scratch_shapes=[
            VMEM((ROWS, HEADS * HEAD), bf),
            VMEM((HEADS, HEAD, ROWS), bf),
            VMEM((ITEMS, KV_HEADS, ROWS, HEAD), bf),
            VMEM((ITEMS, KV_HEADS, VALUE_ROWS, ROWS), bf),
            VMEM((ITEMS, ROWS, ROWS), f32),
            VMEM((HEADS + AT_ONCE, VALUE_ROWS, ROWS), f32),
            VMEM((AT_ONCE, MOST_AT_ONCE, ROWS, ROWS), bf),
            VMEM((HEADS + AT_ONCE, HEAD, ROWS), bf),
            VMEM((8, 1, ROWS), jnp.int32),
            VMEM((HEAD // 2, ROWS), f32),
            VMEM((HEAD // 2, ROWS), f32),
            dma((ITEMS, KV_HEADS)), dma((ITEMS, KV_HEADS)), dma((ITEMS, KV_HEADS)), dma((ITEMS, KV_HEADS)),
            dma((8,)), dma((8,)), dma, dma((HEADS // AT_ONCE,)), dma, dma((ITEMS,)), dma((ITEMS,)),
        ],
        compiler_params=pltpu.CompilerParams(collective_id=0, has_side_effects=True, vmem_limit_bytes=56 * 2**20),
        cost_estimate=pl.CostEstimate(flops=flops, bytes_accessed=12 * 2**20, transcendentals=HEADS * ROWS * ITEMS * ROWS),
        name="attend",
    )(documents.reshape(1, ROWS), inverse, queries, key_projection_rows, value_projection_rows)
    return pl.pallas_call(
        finish,
        grid=(KV_HEADS,),
        out_shape=jax.ShapeDtypeStruct((ROWS, HEADS * HEAD), bf),
        in_specs=[
            pl.BlockSpec((GROUP, HEAD, ROWS), lambda g: (g, 0, 0)),
            pl.BlockSpec((8, ROWS), lambda g: (0, 0)),
            pl.BlockSpec((8, ROWS), lambda g: (0, 0)),
            whole, whole, whole,
        ],
        out_specs=pl.BlockSpec((ROWS, GROUP * HEAD), lambda g: (0, g)),
        scratch_shapes=[
            VMEM((GROUP, HEAD, ROWS), bf),
            VMEM((ITEMS, ROWS, HEAD), bf),
            VMEM((ITEMS, VALUE_ROWS, ROWS), bf),
            dma((3,)),
        ],
        compiler_params=pltpu.CompilerParams(vmem_limit_bytes=40 * 2**20),
        cost_estimate=pl.CostEstimate(flops=2**20, bytes_accessed=4 * 2**20, transcendentals=0),
        name="finish",
    )(o_t, start, bad, q_t, wk, wv)


def solution(mesh):
    in_specs = (
        P(("dp", "ctx")),
        P(("dp", "ctx"), None),
        P(("dp", "ctx"), None),
        P(("dp", "ctx"), None),
    )
    out_specs = P(("dp", "ctx"), None)
    return jax.shard_map(shards, mesh=mesh, in_specs=in_specs, out_specs=out_specs, check_vma=False)
```

profile of v0, /device:TPU:64, one launch (start us, length us, event | category | flops | bytes accessed | tf_op | source)
XLA Modules:
  0.0 225.6 jit_solution(4452566976296047115)
XLA Ops:
  0.0 1.4 jit_solution_.3.inverse
  1.4 49.6 %attend.1 = (bf16[32,128,256]{2,1,0:T(8,128)(2,1)}, bf16[32,128,256]{2,1,0:T(8,128)(2,1)}, bf16[9,4,256,128]{3,2,1,0:T(8,128)(2,1)}, bf16[9,4,144,256]{3,2,1,0:T...) custom-call(s32[1,256]{1,0:T(1,128)} %bitcast.1, f32[64,256]{1,0:T(8,128)} %jit_solution_.3.inverse, ...), custom_call_target="tpu_custom_call" | custom-call | flops 9663676416 | bytes 12582912 | tf_op jit(solution)/shard_map/attend/pallas_call | solution.py:320
  50.9 0.0 copy-start
  51.0 1.7 copy-done
  52.7 0.0 copy-start.1
  52.7 1.7 copy-done.1
  54.4 0.0 copy-start.2
  54.4 1.6 copy-done.2
  56.0 0.0 copy-start.3
  56.0 1.6 copy-done.3
  57.5 0.0 copy-start.4
  57.5 0.7 copy-done.4
  58.2 0.0 copy-start.5
  58.2 0.7 copy-done.5
  58.9 166.7 %finish.1 = bf16[256,4096]{1,0:T(8,128)(2,1)} custom-call(bf16[32,128,256]{2,1,0:T(8,128)(2,1)S(1)} %copy-done.2, f32[8,256]{1,0:T(8,128)S(1)} %copy-done.4, f32[8,256]{1,0:T(8,128)S(1)} %copy-done.5, bf16[32,128,256]{2,1,0:T(8,128)(2,1)S(1)} %copy-done.3, bf16[9,4,256,128]{3,2,1,0:T(8,128)(2,1)S(1)} %copy-done.1, bf16[9,4,144,256]{3,2,1,0:T(8,128)(2,1)S(1)} %copy-done), custom_call_target="tpu_custom_call" | custom-call | flops 1048576 | bytes 4194304 | tf_op jit(solution)/shard_map/finish/pallas_call | solution.py:351
Async XLA Ops:
  50.9 1.8 copy-start
  52.7 1.7 copy-start.1
  54.4 1.6 copy-start.2
  56.0 1.6 copy-start.3
  57.5 0.7 copy-start.4
  58.2 0.7 copy-start.5
where the time goes:
time: 230 us; the launch traced here: 226 us
  Pallas kernels  216 us (94%)
  local copies, waits for them, and re-layouts  9.34 us (4%)
    pallas_call x1, Pallas kernels, shards(): pl.pallas_call(finish, grid=(KV_HEADS,), out_shape=jax.ShapeDtypeStruct((...  167 us
    pallas_call x1, Pallas kernels, shards(): pl.pallas_call(attend, out_shape=[jax.ShapeDtypeStruct((HEADS, HEAD, ROWS...  49.6 us
    unnamed x12, local copies, waits for them, and re-layouts  7.98 us

commit v1 on v0

v1 whole, which is shorter than its diff:
```python
import functools
import math
import jax
import jax.numpy as jnp
import numpy as np
from jax import lax
from jax.experimental import pallas as pl
from jax.experimental.pallas import tpu as pltpu
from jax.sharding import PartitionSpec as P

HEAD = 128
HEADS = 32
KV_HEADS = 4
GROUP = HEADS // KV_HEADS
ROWS = 256
ITEMS = 9
VALUE_ROWS = 144
AT_ONCE = 4
MOST_AT_ONCE = 3
SCALE = math.log2(math.e) / math.sqrt(HEAD)
LOW = 1e-25
HIGH = 1e37
MASKED = -1e30
MESH = pl.DeviceIdType.MESH
VMEM = pltpu.VMEM


def attend(doc_hbm, inverse, q_hbm, k_hbm, v_hbm, out_hbm, qt_hbm, wk_hbm, wv_hbm, start_out, bad_out,
           docs, k_buf, v_buf, q_buf, q_t, wk, wv, bias, acc, probs, doc_win, cosine, sine,
           rk, rv, sk, sv, doc_send, doc_recv, in_sem, out_sem, qt_sem, wk_sem, wv_sem):
    count = lax.axis_size("ctx")
    me = lax.axis_index("ctx")
    x = lax.rem(me, 4)
    row = me - x
    right = row + lax.rem(x + 1, 4)
    left = row + lax.rem(x + 3, 4)
    up = lax.rem(me + 4, count)

    barrier = pltpu.get_barrier_semaphore()

    def greet(other):
        pl.semaphore_signal(barrier, inc=1, device_id={"ctx": other}, device_id_type=MESH)

    for d in range(1, 9):
        @pl.when(d <= me)
        def _():
            greet(lax.rem(me + count - d, count))
    greet(left)
    greet(right)
    loads = [pltpu.make_async_copy(a, b, in_sem.at[n])
             for n, (a, b) in enumerate([(v_hbm, v_buf), (doc_hbm, docs), (k_hbm, k_buf), (q_hbm, q_buf)])]
    for load in loads:
        load.start()

    def value_copy(src, dst, c, target):
        return pltpu.make_async_remote_copy(
            wv.at[src, c, pl.ds(0, HEAD)], wv.at[dst, c, pl.ds(0, HEAD)], sv.at[dst, c], rv.at[dst, c],
            device_id={"ctx": target}, device_id_type=MESH)

    def key_copy(src, dst, c, target):
        return pltpu.make_async_remote_copy(
            wk.at[src, c], wk.at[dst, c], sk.at[dst, c], rk.at[dst, c],
            device_id={"ctx": target}, device_id_type=MESH)

    def doc_copy(d):
        return pltpu.make_async_remote_copy(
            docs, doc_win.at[d - 1], doc_send.at[d - 1], doc_recv.at[d - 1],
            device_id={"ctx": lax.rem(me + d, count)}, device_id_type=MESH)

    def when_sent(condition, copy):
        @pl.when(condition)
        def _():
            copy.start()

    def send_up(copy, src, dst, c):
        when_sent((me + 4 < count) & (src <= me), copy(src, dst, c, up))

    def send_right(copy, src, dst, c, there):
        when_sent(there & (src <= me), copy(src, dst, c, right))

    def send_left(copy, src, dst, c, there):
        when_sent(there & (src <= me), copy(src, dst, c, left))

    wv[:, :, HEAD:, :] = jnp.ones((ITEMS, KV_HEADS, VALUE_ROWS - HEAD, ROWS), jnp.bfloat16)
    loads[0].wait()
    for c in range(KV_HEADS):
        wv[0, c, 0:HEAD] = v_buf[:, c * HEAD:(c + 1) * HEAD].T
    loads[1].wait()
    pl.semaphore_wait(barrier, 2 + jnp.minimum(8, count - 1 - me))
    for d in range(1, 9):
        when_sent(me + d < count, doc_copy(d))
    for c in range(KV_HEADS):
        send_up(value_copy, 0, 4, c)
        send_right(value_copy, 0, 1, c, x < 3)
        send_left(value_copy, 0, 3, c, x == 0)
    loads[3].wait()

    def turn(n, _):
        for u in range(4):
            at = pl.multiple_of((4 * n + u) * HEAD, HEAD)
            q_t[4 * n + u] = q_buf[:, pl.ds(at, HEAD)].T
        return 0

    lax.fori_loop(0, HEADS // 4, turn, 0)
    for d in range(1, 9):
        @pl.when(d > me)
        def _():
            wk[d] = jnp.zeros((KV_HEADS, ROWS, HEAD), jnp.bfloat16)
            wv[d, :, 0:HEAD] = jnp.zeros((KV_HEADS, HEAD, ROWS), jnp.bfloat16)

    doc_row = docs[...].astype(jnp.float32)
    columns = jnp.transpose(jnp.broadcast_to(doc_row, (ROWS, ROWS)))
    local = jnp.sum((columns < doc_row).astype(jnp.float32), axis=0, keepdims=True)
    first = doc_row[:, 0:1]
    powers = jnp.transpose(jnp.broadcast_to(inverse[...], (HEAD, HEAD)))[0:HEAD // 2]
    powers = jnp.concatenate([powers, powers], axis=1)
    tokens = lax.broadcasted_iota(jnp.int32, (1, ROWS), 1).astype(jnp.float32)
    loads[2].wait()
    for d in range(1, 9):
        @pl.when(d <= me)
        def _():
            doc_copy(d).wait_recv()
    behind = jnp.zeros((1, ROWS), jnp.float32)
    for d in range(1, 9):
        same = (doc_win[d - 1].astype(jnp.float32) == first) & (d <= me)
        behind = behind + jnp.where(same, 1.0, 0.0)
    behind = jnp.sum(behind, axis=1, keepdims=True)
    start = jnp.where(doc_row == first, -behind, local)
    start_out[...] = jnp.broadcast_to(start, (8, ROWS))
    angles = powers * (tokens - start)
    cosine[...] = jnp.cos(angles)
    sine[...] = jnp.sin(angles)

    def rotated(matrix):
        wide = matrix.astype(jnp.float32)
        a, b = wide[0:HEAD // 2], wide[HEAD // 2:]
        co, si = cosine[...], sine[...]
        return jnp.concatenate([a * co - b * si, b * co + a * si], axis=0)

    for c in range(KV_HEADS):
        wk[0, c] = rotated(k_buf[:, c * HEAD:(c + 1) * HEAD].T).T.astype(jnp.bfloat16)
    query = lax.broadcasted_iota(jnp.int32, (ROWS, ROWS), 1).astype(jnp.float32)
    key = lax.broadcasted_iota(jnp.int32, (ROWS, ROWS), 0).astype(jnp.float32)
    bias[0] = jnp.where((key >= start) & (key <= query), 0.0, MASKED)
    for c in range(KV_HEADS):
        send_up(key_copy, 0, 4, c)
        send_right(key_copy, 0, 1, c, x < 3)
        send_left(key_copy, 0, 3, c, x == 0)
    for d in range(1, ITEMS):
        at = key - float(ROWS * d)
        bias[d] = jnp.where((at >= start) & (at <= query), 0.0, MASKED)

    def here(values, keys, c):
        for d in values:
            @pl.when(d <= me)
            def _():
                value_copy(d, d, c, up).wait_recv()
        for d in keys:
            @pl.when(d <= me)
            def _():
                key_copy(d, d, c, up).wait_recv()

    def step_one(c, _):
        here((4,), (), c)
        send_right(value_copy, 4, 1, c, x == 3)
        send_left(value_copy, 4, 3, c, x > 0)

        def turned(n, _):
            for u in range(4):
                h = c * GROUP + 4 * n + u
                q_t[h] = rotated(q_t[h]).astype(jnp.bfloat16)
            return 0

        lax.fori_loop(0, GROUP // 4, turned, 0)
        return 0

    lax.fori_loop(0, KV_HEADS, step_one, 0)
    qt_copy = pltpu.make_async_copy(q_t, qt_hbm, qt_sem)
    qt_copy.start()
    bad_out[...] = jnp.zeros((8, ROWS), jnp.float32)

    def weigh(items, at, size):
        for u in range(size):
            h = at + u
            for n, d in enumerate(items):
                scores = lax.dot_general(wk[d, h // GROUP], q_t[h], (((1,), (0,)), ((), ())),
                                         preferred_element_type=jnp.float32)
                probs[u * len(items) + n] = jnp.exp2(scores * SCALE + bias[d]).astype(jnp.bfloat16)

    def gather(items, at, size, begin, end):
        for u in range(size):
            h = at + u
            total = None
            for n, d in enumerate(items):
                part = lax.dot_general(wv[d, h // GROUP], probs[u * len(items) + n], (((1,), (0,)), ((), ())),
                                       preferred_element_type=jnp.float32)
                total = part if total is None else total + part
            if not begin:
                total = acc[h] + total
            if end:
                bottom = total[HEAD:HEAD + 1]
                lane = h * HEAD if isinstance(h, int) else pl.multiple_of(h * HEAD, HEAD)
                q_buf[:, pl.ds(lane, HEAD)] = (total[0:HEAD] * (1.0 / bottom)).astype(jnp.bfloat16).T
                fine = (bottom >= LOW) & (bottom <= HIGH)
                bad_out[0:1] = jnp.maximum(bad_out[0:1], jnp.where(fine, 0.0, 1.0))
            else:
                acc[h] = total

    def out_copy(i):
        wide = AT_ONCE * HEAD
        lanes = pl.ds(i * wide if isinstance(i, int) else pl.multiple_of(i * wide, wide), wide)
        return pltpu.make_async_copy(q_buf.at[:, lanes], out_hbm.at[:, lanes], out_sem.at[i])

    def group(items, size, event, before):
        begin, end = before is None, event is event_six
        per = GROUP // size
        event(0)
        if before is not None:
            gather(before[0], HEADS - before[1], before[1], before[2], False)
        weigh(items, 0, size)

        def inner(i):
            if end:
                @pl.when(i >= 2)
                def _():
                    out_copy(i - 2).start()
            gather(items, size * (i - 1), size, begin, end)
            weigh(items, size * i, size)

        for j in range(1, per):
            inner(j)

        def outer(c, _):
            event(c)
            lax.fori_loop(0, per, lambda j, _: (inner(per * c + j), 0)[1], 0)
            return 0

        lax.fori_loop(1, KV_HEADS, outer, 0)
        return items, size, begin

    def event_two(c):
        here((), (4,), c)
        send_up(value_copy, 4, 8, c)
        send_right(value_copy, 4, 5, c, x < 3)
        send_right(key_copy, 4, 1, c, x == 3)
        send_left(key_copy, 4, 3, c, x > 0)

    def event_three(c):
        here((1, 8), (3,), c)
        send_up(key_copy, 3, 7, c)
        send_right(value_copy, 1, 2, c, x < 3)
        send_right(value_copy, 8, 5, c, x == 3)
        send_left(value_copy, 8, 7, c, x > 0)
        send_left(value_copy, 4, 7, c, x == 0)

    def event_four(c):
        here((3, 5, 7), (1,), c)
        send_up(key_copy, 1, 5, c)
        send_right(key_copy, 1, 2, c, x < 3)
        send_right(value_copy, 5, 2, c, x == 3)
        send_left(value_copy, 7, 6, c, x > 0)
        send_left(value_copy, 3, 6, c, x == 0)

    def event_five(c):
        here((), (5, 7), c)
        send_up(key_copy, 4, 8, c)
        send_right(key_copy, 5, 2, c, x == 3)
        send_left(key_copy, 7, 6, c, x > 0)
        send_left(key_copy, 3, 6, c, x == 0)

    def kept(refs, out, sems, d):
        return pltpu.make_async_copy(refs.at[d], out.at[d], sems.at[d])

    def keep(*items):
        for d in items:
            kept(wk, wk_hbm, wk_sem, d).start()
            kept(wv, wv_hbm, wv_sem, d).start()

    def event_six(c):
        here((2, 6), (2, 6, 8), c)

    before = group((0,), GROUP, event_two, None)
    keep(0)
    before = group((4,), GROUP, event_three, before)
    keep(4)
    before = group((1, 3), AT_ONCE, event_four, before)
    keep(1, 3)
    before = group((5, 7), AT_ONCE, event_five, before)
    keep(5, 7)
    group((2, 6, 8), AT_ONCE, event_six, before)
    keep(2, 6, 8)
    out_copy(6).start()
    gather((2, 6, 8), HEADS - AT_ONCE, AT_ONCE, False, True)
    out_copy(7).start()

    for d in range(1, 9):
        @pl.when(me + d < count)
        def _():
            doc_copy(d).wait_send()

    def drain(c, _):
        for d in range(1, 9):
            if d in (4, 8):
                sent = (me + 4 < count) & (d - 4 <= me)
                sent_key = sent
            elif d in (1, 2):
                sent = jnp.where(x < 3, d - 1, d + 3) <= me
                sent_key = sent
            elif d in (3, 6):
                sent = jnp.where(x > 0, d + 1, d - 3) <= me
                sent_key = sent
            elif d == 5:
                sent = jnp.where(x < 3, d - 1, d + 3) <= me
                sent_key = (me + 4 < count) & (d - 4 <= me)
            else:
                sent = jnp.where(x > 0, d + 1, d - 3) <= me
                sent_key = (me + 4 < count) & (d - 4 <= me)

            @pl.when(sent)
            def _():
                value_copy(d, d, c, up).wait_send()

            @pl.when(sent_key)
            def _():
                key_copy(d, d, c, up).wait_send()
        return 0

    lax.fori_loop(0, KV_HEADS, drain, 0)
    for d in range(ITEMS):
        kept(wk, wk_hbm, wk_sem, d).wait()
        kept(wv, wv_hbm, wv_sem, d).wait()
    qt_copy.wait()
    for i in range(HEADS // AT_ONCE):
        out_copy(i).wait()


def finish(found, start, bad, qt_hbm, wk_hbm, wv_hbm, out, q_buf, k_buf, v_buf, o_buf, sems):
    del found

    @pl.when(jnp.logical_not(jnp.max(bad[...]) < 0.5))
    def _():
        query = lax.broadcasted_iota(jnp.int32, (ROWS, ROWS), 1).astype(jnp.float32)
        key = lax.broadcasted_iota(jnp.int32, (ROWS, ROWS), 0).astype(jnp.float32)
        begin = start[0:1]

        def of_head(h, _):
            copies = [
                pltpu.make_async_copy(qt_hbm.at[h], q_buf, sems.at[0]),
                pltpu.make_async_copy(wk_hbm.at[:, h // GROUP], k_buf, sems.at[1]),
                pltpu.make_async_copy(wv_hbm.at[:, h // GROUP], v_buf, sems.at[2]),
            ]
            for copy in copies:
                copy.start()
            for copy in copies:
                copy.wait()

            def scores(d):
                at = key - (d * ROWS).astype(jnp.float32)
                product = lax.dot_general(k_buf[d], q_buf[...], (((1,), (0,)), ((), ())),
                                          preferred_element_type=jnp.float32)
                return jnp.where((at >= begin) & (at <= query), product * SCALE, MASKED)

            def highest(d, top):
                return jnp.maximum(top, jnp.max(scores(d), axis=0, keepdims=True))

            top = lax.fori_loop(0, ITEMS, highest, jnp.full((1, ROWS), MASKED, jnp.float32))

            def summed(d, carry):
                bottom, total = carry
                weights = jnp.exp2(scores(d) - top)
                bottom = bottom + jnp.sum(weights, axis=0, keepdims=True)
                part = lax.dot_general(v_buf[d, 0:HEAD], weights.astype(jnp.bfloat16), (((1,), (0,)), ((), ())),
                                       preferred_element_type=jnp.float32)
                return bottom, total + part

            bottom, total = lax.fori_loop(
                0, ITEMS, summed, (jnp.zeros((1, ROWS), jnp.float32), jnp.zeros((HEAD, ROWS), jnp.float32)))
            o_buf[...] = (total / bottom).astype(jnp.bfloat16).T
            put = pltpu.make_async_copy(o_buf, out.at[:, pl.ds(pl.multiple_of(h * HEAD, HEAD), HEAD)], sems.at[3])
            put.start()
            put.wait()
            return 0

        lax.fori_loop(0, HEADS, of_head, 0)


def shards(documents, queries, key_projection_rows, value_projection_rows):
    bf, f32 = jnp.bfloat16, jnp.float32
    powers = np.float32(1000000.0) ** (-2.0 * np.arange(HEAD // 2, dtype=np.float32) / HEAD)
    inverse = jnp.asarray(np.tile(powers, 2)[None, :], f32)
    vmem, whole = pl.BlockSpec(memory_space=VMEM), pl.BlockSpec(memory_space=pl.ANY)
    dma = pltpu.SemaphoreType.DMA
    flops = 4 * HEADS * ROWS * ITEMS * ROWS * HEAD
    per_item = (ITEMS, KV_HEADS)
    found, q_t, wk, wv, start, bad = pl.pallas_call(
        attend,
        out_shape=[
            jax.ShapeDtypeStruct((ROWS, HEADS * HEAD), bf),
            jax.ShapeDtypeStruct((HEADS, HEAD, ROWS), bf),
            jax.ShapeDtypeStruct((ITEMS, KV_HEADS, ROWS, HEAD), bf),
            jax.ShapeDtypeStruct((ITEMS, KV_HEADS, VALUE_ROWS, ROWS), bf),
            jax.ShapeDtypeStruct((8, ROWS), f32),
            jax.ShapeDtypeStruct((8, ROWS), f32),
        ],
        in_specs=[whole, vmem, whole, whole, whole],
        out_specs=[whole] * 4 + [vmem] * 2,
        scratch_shapes=[
            VMEM((1, ROWS), jnp.int32),
            VMEM((ROWS, KV_HEADS * HEAD), bf),
            VMEM((ROWS, KV_HEADS * HEAD), bf),
            VMEM((ROWS, HEADS * HEAD), bf),
            VMEM((HEADS, HEAD, ROWS), bf),
            VMEM((ITEMS, KV_HEADS, ROWS, HEAD), bf),
            VMEM((ITEMS, KV_HEADS, VALUE_ROWS, ROWS), bf),
            VMEM((ITEMS, ROWS, ROWS), f32),
            VMEM((HEADS, VALUE_ROWS, ROWS), f32),
            VMEM((AT_ONCE * MOST_AT_ONCE, ROWS, ROWS), bf),
            VMEM((8, 1, ROWS), jnp.int32),
            VMEM((HEAD // 2, ROWS), f32),
            VMEM((HEAD // 2, ROWS), f32),
            dma(per_item), dma(per_item), dma(per_item), dma(per_item),
            dma((8,)), dma((8,)), dma((4,)), dma((HEADS // AT_ONCE,)), dma, dma((ITEMS,)), dma((ITEMS,)),
        ],
        compiler_params=pltpu.CompilerParams(collective_id=0, has_side_effects=True, vmem_limit_bytes=67043328),
        cost_estimate=pl.CostEstimate(flops=flops, bytes_accessed=12 * 2**20, transcendentals=HEADS * ROWS * ITEMS * ROWS),
        name="attend",
    )(documents.reshape(1, ROWS), inverse, queries, key_projection_rows, value_projection_rows)
    return pl.pallas_call(
        finish,
        out_shape=jax.ShapeDtypeStruct((ROWS, HEADS * HEAD), bf),
        in_specs=[whole, vmem, vmem, whole, whole, whole],
        out_specs=whole,
        input_output_aliases={0: 0},
        scratch_shapes=[
            VMEM((HEAD, ROWS), bf),
            VMEM((ITEMS, ROWS, HEAD), bf),
            VMEM((ITEMS, VALUE_ROWS, ROWS), bf),
            VMEM((ROWS, HEAD), bf),
            dma((4,)),
        ],
        compiler_params=pltpu.CompilerParams(vmem_limit_bytes=67043328),
        cost_estimate=pl.CostEstimate(flops=2**20, bytes_accessed=2**14, transcendentals=0),
        name="finish",
    )(found, start, bad, q_t, wk, wv)


def solution(mesh):
    in_specs = (
        P(("dp", "ctx")),
        P(("dp", "ctx"), None),
        P(("dp", "ctx"), None),
        P(("dp", "ctx"), None),
    )
    out_specs = P(("dp", "ctx"), None)
    return jax.shard_map(shards, mesh=mesh, in_specs=in_specs, out_specs=out_specs, check_vma=False)
```

time: 230 us -> 280 us (1.22); the launches traced: 226 us -> 279 us
  Pallas kernels: 216 us -> 275 us
  local copies, waits for them, and re-layouts: 9.34 us -> 3.13 us
    pallas_call x2, Pallas kernels: 216 us -> 275 us  [the longest x1 227 us: shards(): pl.pallas_call(finish, out_shape=jax.ShapeDtypeStruct((ROWS, HEADS * HEAD...]
    unnamed x12 -> x1, local copies, waits for them, and re-layouts: 7.98 us -> 3.13 us
where the time goes in v1:
time: 280 us; the launch traced here: 279 us
  Pallas kernels  275 us (98%)
  local copies, waits for them, and re-layouts  3.13 us (1%)
    pallas_call x1, Pallas kernels, shards(): pl.pallas_call(finish, out_shape=jax.ShapeDtypeStruct((ROWS, HEADS * HEAD...  227 us
    pallas_call x1, Pallas kernels, shards(): pl.pallas_call(attend, out_shape=[jax.ShapeDtypeStruct((ROWS, HEADS * HEA...  48.7 us

profile of v1, /device:TPU:64, one launch (start us, length us, event | category | flops | bytes accessed | tf_op | source)
XLA Modules:
  0.0 278.5 jit_solution(6866543650739264997)
XLA Ops:
  0.0 48.7 %attend.1 = (bf16[256,4096]{1,0:T(8,128)(2,1)}, bf16[32,128,256]{2,1,0:T(8,128)(2,1)}, bf16[9,4,256,128]{3,2,1,0:T(8,128)(2,1)}, bf16[9,4,144,256]{3,2,1,0:T(8,1...) custom-call(s32[1,256]{1,0:T(1,128)} %bitcast.1, f32[1,128]{1,0:T(1,128)} %constant.2.clone.inverse, ...), custom_call_target="tpu_custom_call" | custom-call | flops 9663676416 | bytes 12582912 | tf_op jit(solution)/shard_map/attend/pallas_call | solution.py:395
  48.7 226.7 %finish.1 = bf16[256,4096]{1,0:T(8,128)(2,1)} custom-call(bf16[256,4096]{1,0:T(8,128)(2,1)} %get-tuple-element.11.found, f32[8,256]{1,0:T(8,128)} %get-tuple-element.12.start, f32[8,256]{1,0:T(8,128)} %get-tuple-element.13.bad, bf16[32,128,256]{2,1,0:T(8,128)(2,1)} %get-tuple-element.14.qt_hbm, ...), custom_call_target="tpu_custom_call", output_to_operand_aliasing={{}: (0, {})} | custom-call | flops 1048576 | bytes 16384 | tf_op jit(solution)/shard_map/finish/pallas_call | solution.py:428
  275.4 3.1 %copy.9 = bf16[256,4096]{1,0:T(8,128)(2,1)} copy(bf16[256,4096]{1,0:T(8,128)(2,1)} %finish.1) | data formatting | bytes 4194304

commit v2 on v1

--- a/solution.py
+++ b/solution.py
@@ -22,12 +22,23 @@
 HIGH = 1e37
 MASKED = -1e30
 MESH = pl.DeviceIdType.MESH
+UP, RIGHT, LEFT, RELAY = range(4)
+V, K = range(2)
+SOURCES = {(UP, 4): (0, 0), (UP, 5): (1, 1), (UP, 6): (2, 2), (UP, 7): (3, 3), (UP, 8): (4, 4), (RIGHT, 1): (0, 4),
+           (RIGHT, 2): (1, 5), (RIGHT, 5): (4, 8), (LEFT, 3): (4, 0), (LEFT, 6): (7, 3), (LEFT, 7): (8, 4)}
+ROUTE = {(1, K): RIGHT, (1, V): RIGHT, (2, K): RIGHT, (2, V): RIGHT, (3, K): LEFT, (3, V): LEFT, (4, K): UP, (4, V): UP, (5, K): UP, (5, V): RIGHT, (6, K): LEFT, (6, V): UP, (7, K): LEFT, (7, V): UP, (8, K): RELAY, (8, V): RELAY}
+ARRIVE = {(1, K): (2, 4), (1, V): (1, 9), (2, K): (5, 3), (2, V): (4, 6), (3, K): (3, 2), (3, V): (1, 11), (4, K): (1, 7), (4, V): (0, 14), (5, K): (4, 12), (5, V): (3, 13), (6, K): (5, 15), (6, V): (5, 8), (7, K): (4, 5), (7, V): (3, 0), (8, K): (2, 1), (8, V): (2, 10)}
+LEAVE = {(1, K, 1): 1, (1, V, 1): 0, (2, K, 0): 3, (2, K, 1): 4, (2, V, 0): 2, (2, V, 1): 3, (3, K, 0): 1, (3, V, 0): 0, (5, K, 0): 2, (5, V, 0): 1, (5, V, 1): 2, (6, K, 0): 4, (6, K, 1): 3, (6, V, 0): 4, (7, K, 0): 2, (7, K, 1): 1, (7, V, 0): 1}
+RELAYED = {V: (0, 0), K: (1, 0)}
+RELAY_KEYS_AT = 0
+GROUPS = ((0,), (1, 4), (8,), (5, 3, 7), (2, 6))
+SIZES = (8, 4, 8, 4, 4)
 VMEM = pltpu.VMEM
 
 
 def attend(doc_hbm, inverse, q_hbm, k_hbm, v_hbm, out_hbm, qt_hbm, wk_hbm, wv_hbm, start_out, bad_out,
            docs, k_buf, v_buf, q_buf, q_t, wk, wv, bias, acc, probs, doc_win, cosine, sine,
-           rk, rv, sk, sv, doc_send, doc_recv, in_sem, out_sem, qt_sem, wk_sem, wv_sem):
+           rk, rv, sk, sv, relay_v, relay_k, relay_sems, doc_send, doc_recv, in_sem, out_sem, qt_sem, wk_sem, wv_sem):
     count = lax.axis_size("ctx")
     me = lax.axis_index("ctx")
     x = lax.rem(me, 4)
@@ -36,6 +47,14 @@
     left = row + lax.rem(x + 3, 4)
     up = lax.rem(me + 4, count)
 
+    plane = me - lax.rem(me, 16)
+    y = lax.rem(me // 4, 4)
+    down = plane + 4 * lax.rem(y + 3, 4) + x
+    above = plane + 4 * lax.rem(y + 1, 4) + x
+    behind_8 = me + count - 8
+    far = lax.rem(behind_8, count)
+    relay = far - lax.rem(far, 16) + 4 * lax.rem(lax.rem(far // 4, 4) + 3, 4) + x
+
     barrier = pltpu.get_barrier_semaphore()
 
     def greet(other):
@@ -47,6 +66,15 @@
             greet(lax.rem(me + count - d, count))
     greet(left)
     greet(right)
+
+    @pl.when(above + 8 < count)
+    def _():
+        greet(above)
+
+    @pl.when(me >= 8)
+    def _():
+        greet(relay)
+
     loads = [pltpu.make_async_copy(a, b, in_sem.at[n])
              for n, (a, b) in enumerate([(v_hbm, v_buf), (doc_hbm, docs), (k_hbm, k_buf), (q_hbm, q_buf)])]
     for load in loads:
@@ -72,27 +100,105 @@
         def _():
             copy.start()
 
-    def send_up(copy, src, dst, c):
-        when_sent((me + 4 < count) & (src <= me), copy(src, dst, c, up))
-
-    def send_right(copy, src, dst, c, there):
-        when_sent(there & (src <= me), copy(src, dst, c, right))
-
-    def send_left(copy, src, dst, c, there):
-        when_sent(there & (src <= me), copy(src, dst, c, left))
+    def relay_copy(kind, c):
+        buf = relay_v if kind == V else relay_k
+        mine = wv.at[0, c, pl.ds(0, HEAD)] if kind == V else wk.at[0, c]
+        return pltpu.make_async_remote_copy(
+            mine, buf.at[c], relay_sems.at[kind, 0, c], relay_sems.at[kind, 1, c],
+            device_id={"ctx": down}, device_id_type=MESH)
+
+    def relayed_copy(kind, c):
+        if kind == V:
+            return pltpu.make_async_remote_copy(
+                relay_v.at[c], wv.at[8, c, pl.ds(0, HEAD)], relay_sems.at[kind, 2, c], rv.at[8, c],
+                device_id={"ctx": lax.rem(above + 8, count)}, device_id_type=MESH)
+        return pltpu.make_async_remote_copy(
+            relay_k.at[c], wk.at[8, c], relay_sems.at[kind, 2, c], rk.at[8, c],
+            device_id={"ctx": lax.rem(above + 8, count)}, device_id_type=MESH)
+
+    def relay_own(kind, c):
+        if kind in RELAYED:
+            when_sent(me + 8 < count, relay_copy(kind, c))
+
+    def relay_keys(stage):
+        if K in RELAYED and stage == RELAY_KEYS_AT:
+            for c in range(KV_HEADS):
+                relay_own(K, c)
+
+    def relay_event(stage, late, c):
+        for kind in RELAYED:
+            if RELAYED[kind] == (stage, late):
+                @pl.when(above + 8 < count)
+                def _():
+                    relay_copy(kind, c).wait_recv()
+                    relayed_copy(kind, c).start()
+
+    def drain_relays(c):
+        for kind in RELAYED:
+            @pl.when(me + 8 < count)
+            def _():
+                relay_copy(kind, c).wait_send()
+
+            @pl.when(above + 8 < count)
+            def _():
+                relayed_copy(kind, c).wait_send()
+
+    def copy_of(kind):
+        return value_copy if kind == V else key_copy
+
+    def ways(d, kind):
+        link = ROUTE[d, kind]
+        if link == RELAY:
+            return []
+        plain, edge = SOURCES[link, d]
+        if link == UP:
+            return [(0, plain, up, me + 4 < count)]
+        special = x == 3 if link == RIGHT else x == 0
+        target = right if link == RIGHT else left
+        return [(0, plain, target, jnp.logical_not(special)), (1, edge, target, special)]
+
+    def send(way, d, kind, c):
+        _, src, target, there = way
+        when_sent(there & (src <= me), copy_of(kind)(src, d, c, target))
+
+    def send_own(kind, c):
+        for d in (4, 1, 3):
+            for way in ways(d, kind):
+                if way[1] == 0:
+                    send(way, d, kind, c)
+
+    def stage_event(stage, c):
+        first, after = [], {}
+        for (d, kind) in ROUTE:
+            for way in ways(d, kind):
+                if way[1] != 0 and LEAVE[d, kind, way[0]] == stage:
+                    if ARRIVE[way[1], kind][0] < stage:
+                        first.append((way, d, kind))
+                    else:
+                        after.setdefault((way[1], kind), []).append((way, d, kind))
+        for entry in first:
+            send(*entry, c)
+        relay_event(stage, 0, c)
+        for d, kind in sorted((e for e in ARRIVE if ARRIVE[e][0] == stage), key=lambda e: ARRIVE[e][1]):
+            @pl.when(d <= me)
+            def _():
+                copy_of(kind)(d, d, c, up).wait_recv()
+            for entry in after.get((d, kind), []):
+                send(*entry, c)
+        relay_event(stage, 1, c)
 
     wv[:, :, HEAD:, :] = jnp.ones((ITEMS, KV_HEADS, VALUE_ROWS - HEAD, ROWS), jnp.bfloat16)
     loads[0].wait()
     for c in range(KV_HEADS):
         wv[0, c, 0:HEAD] = v_buf[:, c * HEAD:(c + 1) * HEAD].T
     loads[1].wait()
-    pl.semaphore_wait(barrier, 2 + jnp.minimum(8, count - 1 - me))
+    pl.semaphore_wait(barrier, 2 + jnp.minimum(8, count - 1 - me) + jnp.where(me + 8 < count, 1, 0)
+                      + jnp.where(above + 8 < count, 1, 0))
     for d in range(1, 9):
         when_sent(me + d < count, doc_copy(d))
     for c in range(KV_HEADS):
-        send_up(value_copy, 0, 4, c)
-        send_right(value_copy, 0, 1, c, x < 3)
-        send_left(value_copy, 0, 3, c, x == 0)
+        send_own(V, c)
+        relay_own(V, c)
     loads[3].wait()
 
     def turn(n, _):
@@ -143,27 +249,13 @@
     key = lax.broadcasted_iota(jnp.int32, (ROWS, ROWS), 0).astype(jnp.float32)
     bias[0] = jnp.where((key >= start) & (key <= query), 0.0, MASKED)
     for c in range(KV_HEADS):
-        send_up(key_copy, 0, 4, c)
-        send_right(key_copy, 0, 1, c, x < 3)
-        send_left(key_copy, 0, 3, c, x == 0)
+        send_own(K, c)
     for d in range(1, ITEMS):
         at = key - float(ROWS * d)
         bias[d] = jnp.where((at >= start) & (at <= query), 0.0, MASKED)
 
-    def here(values, keys, c):
-        for d in values:
-            @pl.when(d <= me)
-            def _():
-                value_copy(d, d, c, up).wait_recv()
-        for d in keys:
-            @pl.when(d <= me)
-            def _():
-                key_copy(d, d, c, up).wait_recv()
-
     def step_one(c, _):
-        here((4,), (), c)
-        send_right(value_copy, 4, 1, c, x == 3)
-        send_left(value_copy, 4, 3, c, x > 0)
+        stage_event(0, c)
 
         def turned(n, _):
             for u in range(4):
@@ -174,6 +266,7 @@
         lax.fori_loop(0, GROUP // 4, turned, 0)
         return 0
 
+    relay_keys(0)
     lax.fori_loop(0, KV_HEADS, step_one, 0)
     qt_copy = pltpu.make_async_copy(q_t, qt_hbm, qt_sem)
     qt_copy.start()
@@ -211,10 +304,10 @@
         lanes = pl.ds(i * wide if isinstance(i, int) else pl.multiple_of(i * wide, wide), wide)
         return pltpu.make_async_copy(q_buf.at[:, lanes], out_hbm.at[:, lanes], out_sem.at[i])
 
-    def group(items, size, event, before):
-        begin, end = before is None, event is event_six
+    def group(items, size, stage, before):
+        begin, end = before is None, stage == len(GROUPS)
         per = GROUP // size
-        event(0)
+        stage_event(stage, 0)
         if before is not None:
             gather(before[0], HEADS - before[1], before[1], before[2], False)
         weigh(items, 0, size)
@@ -231,42 +324,12 @@
             inner(j)
 
         def outer(c, _):
-            event(c)
+            stage_event(stage, c)
             lax.fori_loop(0, per, lambda j, _: (inner(per * c + j), 0)[1], 0)
             return 0
 
         lax.fori_loop(1, KV_HEADS, outer, 0)
         return items, size, begin
-
-    def event_two(c):
-        here((), (4,), c)
-        send_up(value_copy, 4, 8, c)
-        send_right(value_copy, 4, 5, c, x < 3)
-        send_right(key_copy, 4, 1, c, x == 3)
-        send_left(key_copy, 4, 3, c, x > 0)
-
-    def event_three(c):
-        here((1, 8), (3,), c)
-        send_up(key_copy, 3, 7, c)
-        send_right(value_copy, 1, 2, c, x < 3)
-        send_right(value_copy, 8, 5, c, x == 3)
-        send_left(value_copy, 8, 7, c, x > 0)
-        send_left(value_copy, 4, 7, c, x == 0)
-
-    def event_four(c):
-        here((3, 5, 7), (1,), c)
-        send_up(key_copy, 1, 5, c)
-        send_right(key_copy, 1, 2, c, x < 3)
-        send_right(value_copy, 5, 2, c, x == 3)
-        send_left(value_copy, 7, 6, c, x > 0)
-        send_left(value_copy, 3, 6, c, x == 0)
-
-    def event_five(c):
-        here((), (5, 7), c)
-        send_up(key_copy, 4, 8, c)
-        send_right(key_copy, 5, 2, c, x == 3)
-        send_left(key_copy, 7, 6, c, x > 0)
-        send_left(key_copy, 3, 6, c, x == 0)
 
     def kept(refs, out, sems, d):
         return pltpu.make_async_copy(refs.at[d], out.at[d], sems.at[d])
@@ -276,21 +339,13 @@
             kept(wk, wk_hbm, wk_sem, d).start()
             kept(wv, wv_hbm, wv_sem, d).start()
 
-    def event_six(c):
-        here((2, 6), (2, 6, 8), c)
-
-    before = group((0,), GROUP, event_two, None)
-    keep(0)
-    before = group((4,), GROUP, event_three, before)
-    keep(4)
-    before = group((1, 3), AT_ONCE, event_four, before)
-    keep(1, 3)
-    before = group((5, 7), AT_ONCE, event_five, before)
-    keep(5, 7)
-    group((2, 6, 8), AT_ONCE, event_six, before)
-    keep(2, 6, 8)
+    before = None
+    for n, items in enumerate(GROUPS):
+        relay_keys(n + 1)
+        before = group(items, SIZES[n], n + 1, before)
+        keep(*items)
     out_copy(6).start()
-    gather((2, 6, 8), HEADS - AT_ONCE, AT_ONCE, False, True)
+    gather(GROUPS[-1], HEADS - AT_ONCE, AT_ONCE, False, True)
     out_copy(7).start()
 
     for d in range(1, 9):
@@ -299,30 +354,12 @@
             doc_copy(d).wait_send()
 
     def drain(c, _):
-        for d in range(1, 9):
-            if d in (4, 8):
-                sent = (me + 4 < count) & (d - 4 <= me)
-                sent_key = sent
-            elif d in (1, 2):
-                sent = jnp.where(x < 3, d - 1, d + 3) <= me
-                sent_key = sent
-            elif d in (3, 6):
-                sent = jnp.where(x > 0, d + 1, d - 3) <= me
-                sent_key = sent
-            elif d == 5:
-                sent = jnp.where(x < 3, d - 1, d + 3) <= me
-                sent_key = (me + 4 < count) & (d - 4 <= me)
-            else:
-                sent = jnp.where(x > 0, d + 1, d - 3) <= me
-                sent_key = (me + 4 < count) & (d - 4 <= me)
-
-            @pl.when(sent)
-            def _():
-                value_copy(d, d, c, up).wait_send()
-
-            @pl.when(sent_key)
-            def _():
-                key_copy(d, d, c, up).wait_send()
+        for (d, kind) in ROUTE:
+            for way in ways(d, kind):
+                @pl.when(way[3] & (way[1] <= me))
+                def _():
+                    copy_of(kind)(d, d, c, up).wait_send()
+        drain_relays(c)
         return 0
 
     lax.fori_loop(0, KV_HEADS, drain, 0)
@@ -334,11 +371,30 @@
         out_copy(i).wait()
 
 
-def finish(found, start, bad, qt_hbm, wk_hbm, wv_hbm, out, q_buf, k_buf, v_buf, o_buf, sems):
-    del found
-
-    @pl.when(jnp.logical_not(jnp.max(bad[...]) < 0.5))
+def finish(found, start, bad, qt_hbm, wk_hbm, wv_hbm, out, o_buf, q_buf, k_buf, v_buf, sems, in_sems, out_sems):
+    pieces = 8
+    tall = ROWS // pieces
+
+    def taken(i):
+        return pltpu.make_async_copy(found.at[pl.ds(i * tall, tall)], o_buf.at[pl.ds(i * tall, tall)], in_sems.at[i])
+
+    def given(i):
+        return pltpu.make_async_copy(o_buf.at[pl.ds(i * tall, tall)], out.at[pl.ds(i * tall, tall)], out_sems.at[i])
+
+    for i in range(pieces):
+        taken(i).start()
+    fine = jnp.max(bad[...]) < 0.5
+
+    @pl.when(fine)
     def _():
+        for i in range(pieces):
+            taken(i).wait()
+            given(i).start()
+
+    @pl.when(jnp.logical_not(fine))
+    def _():
+        for i in range(pieces):
+            taken(i).wait()
         query = lax.broadcasted_iota(jnp.int32, (ROWS, ROWS), 1).astype(jnp.float32)
         key = lax.broadcasted_iota(jnp.int32, (ROWS, ROWS), 0).astype(jnp.float32)
         begin = start[0:1]
@@ -375,13 +431,15 @@
 
             bottom, total = lax.fori_loop(
                 0, ITEMS, summed, (jnp.zeros((1, ROWS), jnp.float32), jnp.zeros((HEAD, ROWS), jnp.float32)))
-            o_buf[...] = (total / bottom).astype(jnp.bfloat16).T
-            put = pltpu.make_async_copy(o_buf, out.at[:, pl.ds(pl.multiple_of(h * HEAD, HEAD), HEAD)], sems.at[3])
-            put.start()
-            put.wait()
+            o_buf[:, pl.ds(pl.multiple_of(h * HEAD, HEAD), HEAD)] = (total / bottom).astype(jnp.bfloat16).T
             return 0
 
         lax.fori_loop(0, HEADS, of_head, 0)
+        for i in range(pieces):
+            given(i).start()
+
+    for i in range(pieces):
+        given(i).wait()
 
 
 def shards(documents, queries, key_projection_rows, value_projection_rows):
@@ -419,6 +477,7 @@
             VMEM((HEAD // 2, ROWS), f32),
             VMEM((HEAD // 2, ROWS), f32),
             dma(per_item), dma(per_item), dma(per_item), dma(per_item),
+            VMEM((KV_HEADS, HEAD, ROWS), bf), VMEM((KV_HEADS, ROWS, HEAD), bf), dma((2, 3, KV_HEADS)),
             dma((8,)), dma((8,)), dma((4,)), dma((HEADS // AT_ONCE,)), dma, dma((ITEMS,)), dma((ITEMS,)),
         ],
         compiler_params=pltpu.CompilerParams(collective_id=0, has_side_effects=True, vmem_limit_bytes=67043328),
@@ -430,13 +489,12 @@
         out_shape=jax.ShapeDtypeStruct((ROWS, HEADS * HEAD), bf),
         in_specs=[whole, vmem, vmem, whole, whole, whole],
         out_specs=whole,
-        input_output_aliases={0: 0},
         scratch_shapes=[
+            VMEM((ROWS, HEADS * HEAD), bf),
             VMEM((HEAD, ROWS), bf),
             VMEM((ITEMS, ROWS, HEAD), bf),
             VMEM((ITEMS, VALUE_ROWS, ROWS), bf),
-            VMEM((ROWS, HEAD), bf),
-            dma((4,)),
+            dma((3,)), dma((8,)), dma((8,)),
         ],
         compiler_params=pltpu.CompilerParams(vmem_limit_bytes=67043328),
         cost_estimate=pl.CostEstimate(flops=2**20, bytes_accessed=2**14, transcendentals=0),

time: 280 us -> 277 us (0.989)
  local copies, waits for them, and re-layouts: 3.13 us -> 0 us
    pallas_call x1, Pallas kernels: 48.7 us -> 66.5 us  [shards(): pl.pallas_call(attend, out_shape=[jax.ShapeDtypeStruct((ROWS, HEADS * HEA...]
    pallas_call x1, Pallas kernels: 227 us -> 209 us  [shards(): pl.pallas_call(finish, out_shape=jax.ShapeDtypeStruct((ROWS, HEADS * HEAD...]
    unnamed x1 -> x0, local copies, waits for them, and re-layouts: 3.13 us -> none
where the time goes in v2:
time: 277 us; the launch traced here: 276 us
  Pallas kernels  276 us (100%)
    pallas_call x1, Pallas kernels, shards(): pl.pallas_call(finish, out_shape=jax.ShapeDtypeStruct((ROWS, HEADS * HEAD...  209 us
    pallas_call x1, Pallas kernels, shards(): pl.pallas_call(attend, out_shape=[jax.ShapeDtypeStruct((ROWS, HEADS * HEA...  66.5 us

profile of v2, /device:TPU:64, one launch (start us, length us, event | category | flops | bytes accessed | tf_op | source)
XLA Modules:
  0.0 275.5 jit_solution(6982094740477637039)
XLA Ops:
  0.0 66.5 %attend.1 = (bf16[256,4096]{1,0:T(8,128)(2,1)}, bf16[32,128,256]{2,1,0:T(8,128)(2,1)}, bf16[9,4,256,128]{3,2,1,0:T(8,128)(2,1)}, bf16[9,4,144,256]{3,2,1,0:T(8,1...) custom-call(s32[1,256]{1,0:T(1,128)} %bitcast.1, f32[1,128]{1,0:T(1,128)} %constant.2.clone.inverse, ...), custom_call_target="tpu_custom_call" | custom-call | flops 9663676416 | bytes 12582912 | tf_op jit(solution)/shard_map/attend/pallas_call | solution.py:453
  66.5 209.0 %finish.1 = bf16[256,4096]{1,0:T(8,128)(2,1)} custom-call(bf16[256,4096]{1,0:T(8,128)(2,1)} %get-tuple-element.11.found, f32[8,256]{1,0:T(8,128)} %get-tuple-element.12.start, f32[8,256]{1,0:T(8,128)} %get-tuple-element.13.bad, bf16[32,128,256]{2,1,0:T(8,128)(2,1)} %get-tuple-element.14.qt_hbm, bf16[9,4,256,128]{3,2,1,0:T(8,128)(2,1)} %get-tuple-element.15.wk_hbm, ...), custom_call_target="tpu_custom_call" | custom-call | flops 1048576 | bytes 16384 | tf_op jit(solution)/shard_map/finish/pallas_call | solution.py:487

commit v3 on v2

--- a/solution.py
+++ b/solution.py
@@ -51,9 +51,8 @@
     y = lax.rem(me // 4, 4)
     down = plane + 4 * lax.rem(y + 3, 4) + x
     above = plane + 4 * lax.rem(y + 1, 4) + x
-    behind_8 = me + count - 8
-    far = lax.rem(behind_8, count)
-    relay = far - lax.rem(far, 16) + 4 * lax.rem(lax.rem(far // 4, 4) + 3, 4) + x
+    ahead = lax.rem(me + 8, count)
+    relay = ahead - lax.rem(ahead, 16) + 4 * lax.rem(lax.rem(ahead // 4, 4) + 1, 4) + x
 
     barrier = pltpu.get_barrier_semaphore()
 
@@ -67,13 +66,13 @@
     greet(left)
     greet(right)
 
-    @pl.when(above + 8 < count)
+    @pl.when(down >= 8)
+    def _():
+        greet(lax.rem(down + count - 8, count))
+
+    @pl.when(me >= 8)
     def _():
         greet(above)
-
-    @pl.when(me >= 8)
-    def _():
-        greet(relay)
 
     loads = [pltpu.make_async_copy(a, b, in_sem.at[n])
              for n, (a, b) in enumerate([(v_hbm, v_buf), (doc_hbm, docs), (k_hbm, k_buf), (q_hbm, q_buf)])]
@@ -105,16 +104,16 @@
         mine = wv.at[0, c, pl.ds(0, HEAD)] if kind == V else wk.at[0, c]
         return pltpu.make_async_remote_copy(
             mine, buf.at[c], relay_sems.at[kind, 0, c], relay_sems.at[kind, 1, c],
-            device_id={"ctx": down}, device_id_type=MESH)
+            device_id={"ctx": relay}, device_id_type=MESH)
 
     def relayed_copy(kind, c):
         if kind == V:
             return pltpu.make_async_remote_copy(
                 relay_v.at[c], wv.at[8, c, pl.ds(0, HEAD)], relay_sems.at[kind, 2, c], rv.at[8, c],
-                device_id={"ctx": lax.rem(above + 8, count)}, device_id_type=MESH)
+                device_id={"ctx": down}, device_id_type=MESH)
         return pltpu.make_async_remote_copy(
             relay_k.at[c], wk.at[8, c], relay_sems.at[kind, 2, c], rk.at[8, c],
-            device_id={"ctx": lax.rem(above + 8, count)}, device_id_type=MESH)
+            device_id={"ctx": down}, device_id_type=MESH)
 
     def relay_own(kind, c):
         if kind in RELAYED:
@@ -128,7 +127,7 @@
     def relay_event(stage, late, c):
         for kind in RELAYED:
             if RELAYED[kind] == (stage, late):
-                @pl.when(above + 8 < count)
+                @pl.when(down >= 8)
                 def _():
                     relay_copy(kind, c).wait_recv()
                     relayed_copy(kind, c).start()
@@ -139,7 +138,7 @@
             def _():
                 relay_copy(kind, c).wait_send()
 
-            @pl.when(above + 8 < count)
+            @pl.when(down >= 8)
             def _():
                 relayed_copy(kind, c).wait_send()
 
@@ -193,7 +192,7 @@
         wv[0, c, 0:HEAD] = v_buf[:, c * HEAD:(c + 1) * HEAD].T
     loads[1].wait()
     pl.semaphore_wait(barrier, 2 + jnp.minimum(8, count - 1 - me) + jnp.where(me + 8 < count, 1, 0)
-                      + jnp.where(above + 8 < count, 1, 0))
+                      + jnp.where(down >= 8, 1, 0))
     for d in range(1, 9):
         when_sent(me + d < count, doc_copy(d))
     for c in range(KV_HEADS):

time: 277 us -> 262 us (0.946)
  Pallas kernels: 276 us -> 261 us
    pallas_call x1, Pallas kernels: 66.5 us -> 51.8 us  [shards(): pl.pallas_call(attend, out_shape=[jax.ShapeDtypeStruct((ROWS, HEADS * HEA...]
where the time goes in v3:
time: 262 us; the launch traced here: 261 us
  Pallas kernels  261 us (100%)
    pallas_call x1, Pallas kernels, shards(): pl.pallas_call(finish, out_shape=jax.ShapeDtypeStruct((ROWS, HEADS * HEAD...  209 us
    pallas_call x1, Pallas kernels, shards(): pl.pallas_call(attend, out_shape=[jax.ShapeDtypeStruct((ROWS, HEADS * HEA...  51.8 us

profile of v3, /device:TPU:64, one launch (start us, length us, event | category | flops | bytes accessed | tf_op | source)
XLA Modules:
  0.0 260.9 jit_solution(4356103716289840210)
XLA Ops:
  0.0 51.8 %attend.1 = (bf16[256,4096]{1,0:T(8,128)(2,1)}, bf16[32,128,256]{2,1,0:T(8,128)(2,1)}, bf16[9,4,256,128]{3,2,1,0:T(8,128)(2,1)}, bf16[9,4,144,256]{3,2,1,0:T(8,1...) custom-call(s32[1,256]{1,0:T(1,128)} %bitcast.1, f32[1,128]{1,0:T(1,128)} %constant.2.clone.inverse, ...), custom_call_target="tpu_custom_call" | custom-call | flops 9663676416 | bytes 12582912 | tf_op jit(solution)/shard_map/attend/pallas_call | solution.py:452
  51.9 209.1 %finish.1 = bf16[256,4096]{1,0:T(8,128)(2,1)} custom-call(bf16[256,4096]{1,0:T(8,128)(2,1)} %get-tuple-element.11.found, f32[8,256]{1,0:T(8,128)} %get-tuple-element.12.start, f32[8,256]{1,0:T(8,128)} %get-tuple-element.13.bad, bf16[32,128,256]{2,1,0:T(8,128)(2,1)} %get-tuple-element.14.qt_hbm, bf16[9,4,256,128]{3,2,1,0:T(8,128)(2,1)} %get-tuple-element.15.wk_hbm, ...), custom_call_target="tpu_custom_call" | custom-call | flops 1048576 | bytes 16384 | tf_op jit(solution)/shard_map/finish/pallas_call | solution.py:486

commit v4 on v3

--- a/solution.py
+++ b/solution.py
@@ -26,13 +26,13 @@
 V, K = range(2)
 SOURCES = {(UP, 4): (0, 0), (UP, 5): (1, 1), (UP, 6): (2, 2), (UP, 7): (3, 3), (UP, 8): (4, 4), (RIGHT, 1): (0, 4),
            (RIGHT, 2): (1, 5), (RIGHT, 5): (4, 8), (LEFT, 3): (4, 0), (LEFT, 6): (7, 3), (LEFT, 7): (8, 4)}
-ROUTE = {(1, K): RIGHT, (1, V): RIGHT, (2, K): RIGHT, (2, V): RIGHT, (3, K): LEFT, (3, V): LEFT, (4, K): UP, (4, V): UP, (5, K): UP, (5, V): RIGHT, (6, K): LEFT, (6, V): UP, (7, K): LEFT, (7, V): UP, (8, K): RELAY, (8, V): RELAY}
-ARRIVE = {(1, K): (2, 4), (1, V): (1, 9), (2, K): (5, 3), (2, V): (4, 6), (3, K): (3, 2), (3, V): (1, 11), (4, K): (1, 7), (4, V): (0, 14), (5, K): (4, 12), (5, V): (3, 13), (6, K): (5, 15), (6, V): (5, 8), (7, K): (4, 5), (7, V): (3, 0), (8, K): (2, 1), (8, V): (2, 10)}
-LEAVE = {(1, K, 1): 1, (1, V, 1): 0, (2, K, 0): 3, (2, K, 1): 4, (2, V, 0): 2, (2, V, 1): 3, (3, K, 0): 1, (3, V, 0): 0, (5, K, 0): 2, (5, V, 0): 1, (5, V, 1): 2, (6, K, 0): 4, (6, K, 1): 3, (6, V, 0): 4, (7, K, 0): 2, (7, K, 1): 1, (7, V, 0): 1}
-RELAYED = {V: (0, 0), K: (1, 0)}
-RELAY_KEYS_AT = 0
-GROUPS = ((0,), (1, 4), (8,), (5, 3, 7), (2, 6))
-SIZES = (8, 4, 8, 4, 4)
+ROUTE = {(1, K, 0): RIGHT, (1, K, 1): RIGHT, (1, V, 0): RIGHT, (1, V, 1): RIGHT, (2, K, 0): RIGHT, (2, K, 1): RIGHT, (2, V, 0): RIGHT, (2, V, 1): RIGHT, (3, K, 0): LEFT, (3, K, 1): LEFT, (3, V, 0): LEFT, (3, V, 1): LEFT, (4, K, 0): UP, (4, K, 1): UP, (4, V, 0): UP, (4, V, 1): UP, (5, K, 0): UP, (5, K, 1): UP, (5, V, 0): RIGHT, (5, V, 1): UP, (6, K, 0): UP, (6, K, 1): UP, (6, V, 0): LEFT, (6, V, 1): LEFT, (7, K, 0): UP, (7, K, 1): UP, (7, V, 0): LEFT, (7, V, 1): LEFT, (8, K, 0): RELAY, (8, K, 1): RELAY, (8, V, 0): RELAY, (8, V, 1): RELAY}
+ARRIVE = {(1, K): (2, 3), (1, V): (1, 0), (2, K): (4, 11), (2, V): (5, 15), (3, K): (3, 13), (3, V): (2, 4), (4, K): (1, 10), (4, V): (0, 1), (5, K): (3, 9), (5, V): (3, 2), (6, K): (5, 7), (6, V): (5, 5), (7, K): (4, 6), (7, V): (4, 8), (8, K): (4, 12), (8, V): (2, 14)}
+LEAVE = {(1, K, 0, 1): 1, (1, K, 1, 1): 1, (1, V, 0, 1): 0, (1, V, 1, 1): 0, (2, K, 0, 0): 2, (2, K, 0, 1): 3, (2, K, 1, 0): 2, (2, K, 1, 1): 3, (2, V, 0, 0): 3, (2, V, 0, 1): 4, (2, V, 1, 0): 3, (2, V, 1, 1): 4, (3, K, 0, 0): 1, (3, K, 1, 0): 1, (3, V, 0, 0): 0, (3, V, 1, 0): 0, (5, K, 0, 0): 2, (5, K, 1, 0): 2, (5, V, 0, 0): 0, (5, V, 0, 1): 2, (5, V, 1, 0): 1, (6, K, 0, 0): 4, (6, K, 1, 0): 4, (6, V, 0, 0): 4, (6, V, 0, 1): 2, (6, V, 1, 0): 4, (6, V, 1, 1): 2, (7, K, 0, 0): 3, (7, K, 1, 0): 3, (7, V, 0, 0): 2, (7, V, 0, 1): 0, (7, V, 1, 0): 2, (7, V, 1, 1): 0}
+RELAYED = {V: (0, 0), K: (3, 1)}
+RELAY_KEYS_AT = 1
+GROUPS = ((0,), (1, 4), (3, 5), (8,), (2, 6, 7))
+SIZES = (8, 4, 4, 8, 4)
 VMEM = pltpu.VMEM
 
 
@@ -145,8 +145,8 @@
     def copy_of(kind):
         return value_copy if kind == V else key_copy
 
-    def ways(d, kind):
-        link = ROUTE[d, kind]
+    def ways(d, kind, half):
+        link = ROUTE[d, kind, half]
         if link == RELAY:
             return []
         plain, edge = SOURCES[link, d]
@@ -156,25 +156,33 @@
         target = right if link == RIGHT else left
         return [(0, plain, target, jnp.logical_not(special)), (1, edge, target, special)]
 
-    def send(way, d, kind, c):
+    def send(way, d, kind, half, c):
         _, src, target, there = way
+        if ROUTE[d, kind, 1 - half] != ROUTE[d, kind, half]:
+            if isinstance(c, int):
+                if c // 2 != half:
+                    return
+            else:
+                there = there & (c // 2 == half)
+        elif half:
+            return
         when_sent(there & (src <= me), copy_of(kind)(src, d, c, target))
 
     def send_own(kind, c):
         for d in (4, 1, 3):
-            for way in ways(d, kind):
+            for way in ways(d, kind, 0):
                 if way[1] == 0:
-                    send(way, d, kind, c)
+                    send(way, d, kind, 0, c)
 
     def stage_event(stage, c):
         first, after = [], {}
-        for (d, kind) in ROUTE:
-            for way in ways(d, kind):
-                if way[1] != 0 and LEAVE[d, kind, way[0]] == stage:
+        for (d, kind, half) in ROUTE:
+            for way in ways(d, kind, half):
+                if way[1] != 0 and LEAVE[d, kind, half, way[0]] == stage:
                     if ARRIVE[way[1], kind][0] < stage:
-                        first.append((way, d, kind))
+                        first.append((way, d, kind, half))
                     else:
-                        after.setdefault((way[1], kind), []).append((way, d, kind))
+                        after.setdefault((way[1], kind), []).append((way, d, kind, half))
         for entry in first:
             send(*entry, c)
         relay_event(stage, 0, c)
@@ -353,9 +361,10 @@
             doc_copy(d).wait_send()
 
     def drain(c, _):
-        for (d, kind) in ROUTE:
-            for way in ways(d, kind):
-                @pl.when(way[3] & (way[1] <= me))
+        for (d, kind, half) in ROUTE:
+            same = ROUTE[d, kind, 1 - half] == ROUTE[d, kind, half]
+            for way in ways(d, kind, half) if not (same and half) else []:
+                @pl.when(way[3] & (way[1] <= me) & ((c // 2 == half) | same))
                 def _():
                     copy_of(kind)(d, d, c, up).wait_send()
         drain_relays(c)
@@ -370,7 +379,7 @@
         out_copy(i).wait()
 
 
-def finish(found, start, bad, qt_hbm, wk_hbm, wv_hbm, out, o_buf, q_buf, k_buf, v_buf, sems, in_sems, out_sems):
+def finish(found, start_hbm, bad_hbm, qt_hbm, wk_hbm, wv_hbm, out, o_buf, start, bad, q_buf, k_buf, v_buf, sems, in_sems, out_sems):
     pieces = 8
     tall = ROWS // pieces
 
@@ -380,8 +389,13 @@
     def given(i):
         return pltpu.make_async_copy(o_buf.at[pl.ds(i * tall, tall)], out.at[pl.ds(i * tall, tall)], out_sems.at[i])
 
+    small = [pltpu.make_async_copy(bad_hbm, bad, sems.at[3]), pltpu.make_async_copy(start_hbm, start, sems.at[4])]
+    for copy in small:
+        copy.start()
     for i in range(pieces):
         taken(i).start()
+    for copy in small:
+        copy.wait()
     fine = jnp.max(bad[...]) < 0.5
 
     @pl.when(fine)
@@ -486,14 +500,16 @@
     return pl.pallas_call(
         finish,
         out_shape=jax.ShapeDtypeStruct((ROWS, HEADS * HEAD), bf),
-        in_specs=[whole, vmem, vmem, whole, whole, whole],
+        in_specs=[whole] * 6,
         out_specs=whole,
         scratch_shapes=[
             VMEM((ROWS, HEADS * HEAD), bf),
+            VMEM((8, ROWS), f32),
+            VMEM((8, ROWS), f32),
             VMEM((HEAD, ROWS), bf),
             VMEM((ITEMS, ROWS, HEAD), bf),
             VMEM((ITEMS, VALUE_ROWS, ROWS), bf),
-            dma((3,)), dma((8,)), dma((8,)),
+            dma((5,)), dma((8,)), dma((8,)),
         ],
         compiler_params=pltpu.CompilerParams(vmem_limit_bytes=67043328),
         cost_estimate=pl.CostEstimate(flops=2**20, bytes_accessed=2**14, transcendentals=0),

time: 262 us -> 256 us (0.977)
  Pallas kernels: 261 us -> 255 us
    pallas_call x1, Pallas kernels: 51.8 us -> 46.7 us  [shards(): pl.pallas_call(attend, out_shape=[jax.ShapeDtypeStruct((ROWS, HEADS * HEA...]
where the time goes in v4:
time: 256 us; the launch traced here: 255 us
  Pallas kernels  255 us (100%)
    pallas_call x1, Pallas kernels, shards(): pl.pallas_call(finish, out_shape=jax.ShapeDtypeStruct((ROWS, HEADS * HEAD...  208 us
    pallas_call x1, Pallas kernels, shards(): pl.pallas_call(attend, out_shape=[jax.ShapeDtypeStruct((ROWS, HEADS * HEA...  46.7 us

profile of v4, /device:TPU:64, one launch (start us, length us, event | category | flops | bytes accessed | tf_op | source)
XLA Modules:
  0.0 255.1 jit_solution(169080750014205941)
XLA Ops:
  0.0 46.7 %attend.1 = (bf16[256,4096]{1,0:T(8,128)(2,1)}, bf16[32,128,256]{2,1,0:T(8,128)(2,1)}, bf16[9,4,256,128]{3,2,1,0:T(8,128)(2,1)}, bf16[9,4,144,256]{3,2,1,0:T(8,1...) custom-call(s32[1,256]{1,0:T(1,128)} %bitcast.1, f32[1,128]{1,0:T(1,128)} %constant.2.clone.inverse, ...), custom_call_target="tpu_custom_call" | custom-call | flops 9663676416 | bytes 12582912 | tf_op jit(solution)/shard_map/attend/pallas_call | solution.py:466
  46.7 208.4 %finish.1 = bf16[256,4096]{1,0:T(8,128)(2,1)} custom-call(bf16[256,4096]{1,0:T(8,128)(2,1)} %get-tuple-element.11.found, f32[8,256]{1,0:T(8,128)} %get-tuple-element.12.start_hbm, f32[8,256]{1,0:T(8,128)} %get-tuple-element.13.bad_hbm, bf16[32,128,256]{2,1,0:T(8,128)(2,1)} %get-tuple-element.14.qt_hbm, bf16[9,4,256,128]{3,2,1,0:T(8,128)(2,1)} %get-tuple-element.15.wk_hbm, ...), custom_call_target="tpu_custom_call" | custom-call | flops 1048576 | bytes 16384 | tf_op jit(solution)/shard_map/finish/pallas_call | solution.py:500

commit v5 on v4

--- a/solution.py
+++ b/solution.py
@@ -27,18 +27,18 @@
 SOURCES = {(UP, 4): (0, 0), (UP, 5): (1, 1), (UP, 6): (2, 2), (UP, 7): (3, 3), (UP, 8): (4, 4), (RIGHT, 1): (0, 4),
            (RIGHT, 2): (1, 5), (RIGHT, 5): (4, 8), (LEFT, 3): (4, 0), (LEFT, 6): (7, 3), (LEFT, 7): (8, 4)}
 ROUTE = {(1, K, 0): RIGHT, (1, K, 1): RIGHT, (1, V, 0): RIGHT, (1, V, 1): RIGHT, (2, K, 0): RIGHT, (2, K, 1): RIGHT, (2, V, 0): RIGHT, (2, V, 1): RIGHT, (3, K, 0): LEFT, (3, K, 1): LEFT, (3, V, 0): LEFT, (3, V, 1): LEFT, (4, K, 0): UP, (4, K, 1): UP, (4, V, 0): UP, (4, V, 1): UP, (5, K, 0): UP, (5, K, 1): UP, (5, V, 0): RIGHT, (5, V, 1): UP, (6, K, 0): UP, (6, K, 1): UP, (6, V, 0): LEFT, (6, V, 1): LEFT, (7, K, 0): UP, (7, K, 1): UP, (7, V, 0): LEFT, (7, V, 1): LEFT, (8, K, 0): RELAY, (8, K, 1): RELAY, (8, V, 0): RELAY, (8, V, 1): RELAY}
-ARRIVE = {(1, K): (2, 3), (1, V): (1, 0), (2, K): (4, 11), (2, V): (5, 15), (3, K): (3, 13), (3, V): (2, 4), (4, K): (1, 10), (4, V): (0, 1), (5, K): (3, 9), (5, V): (3, 2), (6, K): (5, 7), (6, V): (5, 5), (7, K): (4, 6), (7, V): (4, 8), (8, K): (4, 12), (8, V): (2, 14)}
-LEAVE = {(1, K, 0, 1): 1, (1, K, 1, 1): 1, (1, V, 0, 1): 0, (1, V, 1, 1): 0, (2, K, 0, 0): 2, (2, K, 0, 1): 3, (2, K, 1, 0): 2, (2, K, 1, 1): 3, (2, V, 0, 0): 3, (2, V, 0, 1): 4, (2, V, 1, 0): 3, (2, V, 1, 1): 4, (3, K, 0, 0): 1, (3, K, 1, 0): 1, (3, V, 0, 0): 0, (3, V, 1, 0): 0, (5, K, 0, 0): 2, (5, K, 1, 0): 2, (5, V, 0, 0): 0, (5, V, 0, 1): 2, (5, V, 1, 0): 1, (6, K, 0, 0): 4, (6, K, 1, 0): 4, (6, V, 0, 0): 4, (6, V, 0, 1): 2, (6, V, 1, 0): 4, (6, V, 1, 1): 2, (7, K, 0, 0): 3, (7, K, 1, 0): 3, (7, V, 0, 0): 2, (7, V, 0, 1): 0, (7, V, 1, 0): 2, (7, V, 1, 1): 0}
-RELAYED = {V: (0, 0), K: (3, 1)}
+ARRIVE = {(1, K): (2, 11), (1, V): (1, 6), (2, K): (4, 12), (2, V): (5, 4), (3, K): (3, 8), (3, V): (2, 9), (4, K): (1, 14), (4, V): (0, 3), (5, K): (3, 7), (5, V): (4, 13), (6, K): (6, 1), (6, V): (6, 2), (7, K): (4, 15), (7, V): (4, 10), (8, K): (4, 0), (8, V): (2, 5)}
+LEAVE = {(1, K, 0, 1): 1, (1, K, 1, 1): 1, (1, V, 0, 1): 0, (1, V, 1, 1): 0, (2, K, 0, 0): 2, (2, K, 0, 1): 3, (2, K, 1, 0): 2, (2, K, 1, 1): 3, (2, V, 0, 0): 1, (2, V, 0, 1): 4, (2, V, 1, 0): 1, (2, V, 1, 1): 4, (3, K, 0, 0): 1, (3, K, 1, 0): 1, (3, V, 0, 0): 0, (3, V, 1, 0): 0, (5, K, 0, 0): 2, (5, K, 1, 0): 2, (5, V, 0, 0): 1, (5, V, 0, 1): 2, (5, V, 1, 0): 1, (6, K, 0, 0): 4, (6, K, 1, 0): 4, (6, V, 0, 0): 4, (6, V, 0, 1): 2, (6, V, 1, 0): 4, (6, V, 1, 1): 2, (7, K, 0, 0): 3, (7, K, 1, 0): 3, (7, V, 0, 0): 2, (7, V, 0, 1): 0, (7, V, 1, 0): 2, (7, V, 1, 1): 0}
+RELAYED = {V: (0, 1), K: (3, 1)}
 RELAY_KEYS_AT = 1
-GROUPS = ((0,), (1, 4), (3, 5), (8,), (2, 6, 7))
-SIZES = (8, 4, 4, 8, 4)
+GROUPS = ((0,), (4,), (3, 1), (5, 8, 7), (2,), (6,))
+SIZES = (8, 8, 4, 4, 8, 8)
 VMEM = pltpu.VMEM
 
 
-def attend(doc_hbm, inverse, q_hbm, k_hbm, v_hbm, out_hbm, qt_hbm, wk_hbm, wv_hbm, start_out, bad_out,
-           docs, k_buf, v_buf, q_buf, q_t, wk, wv, bias, acc, probs, doc_win, cosine, sine,
-           rk, rv, sk, sv, relay_v, relay_k, relay_sems, doc_send, doc_recv, in_sem, out_sem, qt_sem, wk_sem, wv_sem):
+def attend(doc_hbm, inverse_hbm, q_hbm, k_hbm, v_hbm, out_hbm, qt_hbm, wk_hbm, wv_hbm, start_hbm, bad_hbm,
+           inverse, start_out, bad_out, docs, k_buf, v_buf, q_buf, q_t, wk, wv, bias, acc, probs, doc_win, cosine, sine,
+           rk, rv, sk, sv, relay_v, relay_k, relay_sems, doc_send, doc_recv, in_sem, out_sem, qt_sem, wk_sem, wv_sem, small_sem):
     count = lax.axis_size("ctx")
     me = lax.axis_index("ctx")
     x = lax.rem(me, 4)
@@ -75,7 +75,8 @@
         greet(above)
 
     loads = [pltpu.make_async_copy(a, b, in_sem.at[n])
-             for n, (a, b) in enumerate([(v_hbm, v_buf), (doc_hbm, docs), (k_hbm, k_buf), (q_hbm, q_buf)])]
+             for n, (a, b) in enumerate([(v_hbm, v_buf), (doc_hbm, docs), (k_hbm, k_buf), (q_hbm, q_buf),
+                                    (inverse_hbm, inverse)])]
     for load in loads:
         load.start()
 
@@ -225,6 +226,7 @@
     columns = jnp.transpose(jnp.broadcast_to(doc_row, (ROWS, ROWS)))
     local = jnp.sum((columns < doc_row).astype(jnp.float32), axis=0, keepdims=True)
     first = doc_row[:, 0:1]
+    loads[4].wait()
     powers = jnp.transpose(jnp.broadcast_to(inverse[...], (HEAD, HEAD)))[0:HEAD // 2]
     powers = jnp.concatenate([powers, powers], axis=1)
     tokens = lax.broadcasted_iota(jnp.int32, (1, ROWS), 1).astype(jnp.float32)
@@ -277,6 +279,8 @@
     lax.fori_loop(0, KV_HEADS, step_one, 0)
     qt_copy = pltpu.make_async_copy(q_t, qt_hbm, qt_sem)
     qt_copy.start()
+    start_copy = pltpu.make_async_copy(start_out, start_hbm, small_sem.at[0])
+    start_copy.start()
     bad_out[...] = jnp.zeros((8, ROWS), jnp.float32)
 
     def weigh(items, at, size):
@@ -307,7 +311,7 @@
                 acc[h] = total
 
     def out_copy(i):
-        wide = AT_ONCE * HEAD
+        wide = SIZES[-1] * HEAD
         lanes = pl.ds(i * wide if isinstance(i, int) else pl.multiple_of(i * wide, wide), wide)
         return pltpu.make_async_copy(q_buf.at[:, lanes], out_hbm.at[:, lanes], out_sem.at[i])
 
@@ -351,9 +355,12 @@
         relay_keys(n + 1)
         before = group(items, SIZES[n], n + 1, before)
         keep(*items)
-    out_copy(6).start()
-    gather(GROUPS[-1], HEADS - AT_ONCE, AT_ONCE, False, True)
-    out_copy(7).start()
+    batches = HEADS // SIZES[-1]
+    out_copy(batches - 2).start()
+    gather(GROUPS[-1], HEADS - SIZES[-1], SIZES[-1], False, True)
+    out_copy(batches - 1).start()
+    bad_copy = pltpu.make_async_copy(bad_out, bad_hbm, small_sem.at[1])
+    bad_copy.start()
 
     for d in range(1, 9):
         @pl.when(me + d < count)
@@ -375,7 +382,9 @@
         kept(wk, wk_hbm, wk_sem, d).wait()
         kept(wv, wv_hbm, wv_sem, d).wait()
     qt_copy.wait()
-    for i in range(HEADS // AT_ONCE):
+    start_copy.wait()
+    bad_copy.wait()
+    for i in range(batches):
         out_copy(i).wait()
 
 
@@ -459,7 +468,7 @@
     bf, f32 = jnp.bfloat16, jnp.float32
     powers = np.float32(1000000.0) ** (-2.0 * np.arange(HEAD // 2, dtype=np.float32) / HEAD)
     inverse = jnp.asarray(np.tile(powers, 2)[None, :], f32)
-    vmem, whole = pl.BlockSpec(memory_space=VMEM), pl.BlockSpec(memory_space=pl.ANY)
+    whole = pl.BlockSpec(memory_space=pl.ANY)
     dma = pltpu.SemaphoreType.DMA
     flops = 4 * HEADS * ROWS * ITEMS * ROWS * HEAD
     per_item = (ITEMS, KV_HEADS)
@@ -473,9 +482,12 @@
             jax.ShapeDtypeStruct((8, ROWS), f32),
             jax.ShapeDtypeStruct((8, ROWS), f32),
         ],
-        in_specs=[whole, vmem, whole, whole, whole],
-        out_specs=[whole] * 4 + [vmem] * 2,
+        in_specs=[whole] * 5,
+        out_specs=[whole] * 6,
         scratch_shapes=[
+            VMEM((1, HEAD), f32),
+            VMEM((8, ROWS), f32),
+            VMEM((8, ROWS), f32),
             VMEM((1, ROWS), jnp.int32),
             VMEM((ROWS, KV_HEADS * HEAD), bf),
             VMEM((ROWS, KV_HEADS * HEAD), bf),
@@ -491,7 +503,7 @@
             VMEM((HEAD // 2, ROWS), f32),
             dma(per_item), dma(per_item), dma(per_item), dma(per_item),
             VMEM((KV_HEADS, HEAD, ROWS), bf), VMEM((KV_HEADS, ROWS, HEAD), bf), dma((2, 3, KV_HEADS)),
-            dma((8,)), dma((8,)), dma((4,)), dma((HEADS // AT_ONCE,)), dma, dma((ITEMS,)), dma((ITEMS,)),
+            dma((8,)), dma((8,)), dma((5,)), dma((HEADS // AT_ONCE,)), dma, dma((ITEMS,)), dma((ITEMS,)), dma((2,)),
         ],
         compiler_params=pltpu.CompilerParams(collective_id=0, has_side_effects=True, vmem_limit_bytes=67043328),
         cost_estimate=pl.CostEstimate(flops=flops, bytes_accessed=12 * 2**20, transcendentals=HEADS * ROWS * ITEMS * ROWS),

time: 256 us -> 255 us (level)
  no operation moved by 1% of the time
where the time goes in v5:
time: 255 us; the launch traced here: 254 us
  Pallas kernels  254 us (100%)
    pallas_call x1, Pallas kernels, shards(): pl.pallas_call(finish, out_shape=jax.ShapeDtypeStruct((ROWS, HEADS * HEAD...  208 us
    pallas_call x1, Pallas kernels, shards(): pl.pallas_call(attend, out_shape=[jax.ShapeDtypeStruct((ROWS, HEADS * HEA...  45.3 us

profile of v5, /device:TPU:64, one launch (start us, length us, event | category | flops | bytes accessed | tf_op | source)
XLA Modules:
  0.0 253.6 jit_solution(10759940924398194607)
XLA Ops:
  0.0 45.3 %attend.1 = (bf16[256,4096]{1,0:T(8,128)(2,1)}, bf16[32,128,256]{2,1,0:T(8,128)(2,1)}, bf16[9,4,256,128]{3,2,1,0:T(8,128)(2,1)}, bf16[9,4,144,256]{3,2,1,0:T(8,1...) custom-call(s32[1,256]{1,0:T(1,128)} %bitcast.1, f32[1,128]{1,0:T(1,128)} %constant.2.clone.inverse_hbm, ...), custom_call_target="tpu_custom_call" | custom-call | flops 9663676416 | bytes 12582912 | tf_op jit(solution)/shard_map/attend/pallas_call | solution.py:475
  45.3 208.4 %finish.1 = bf16[256,4096]{1,0:T(8,128)(2,1)} custom-call(bf16[256,4096]{1,0:T(8,128)(2,1)} %get-tuple-element.11.found, f32[8,256]{1,0:T(8,128)} %get-tuple-element.12.start_hbm, f32[8,256]{1,0:T(8,128)} %get-tuple-element.13.bad_hbm, bf16[32,128,256]{2,1,0:T(8,128)(2,1)} %get-tuple-element.14.qt_hbm, bf16[9,4,256,128]{3,2,1,0:T(8,128)(2,1)} %get-tuple-element.15.wk_hbm, ...), custom_call_target="tpu_custom_call" | custom-call | flops 1048576 | bytes 16384 | tf_op jit(solution)/shard_map/finish/pallas_call | solution.py:512

commit v6 on v5

--- a/solution.py
+++ b/solution.py
@@ -22,13 +22,37 @@
 HIGH = 1e37
 MASKED = -1e30
 MESH = pl.DeviceIdType.MESH
-UP, RIGHT, LEFT, RELAY = range(4)
+UP, RIGHT, LEFT = range(3)
 V, K = range(2)
-SOURCES = {(UP, 4): (0, 0), (UP, 5): (1, 1), (UP, 6): (2, 2), (UP, 7): (3, 3), (UP, 8): (4, 4), (RIGHT, 1): (0, 4),
-           (RIGHT, 2): (1, 5), (RIGHT, 5): (4, 8), (LEFT, 3): (4, 0), (LEFT, 6): (7, 3), (LEFT, 7): (8, 4)}
-ROUTE = {(1, K, 0): RIGHT, (1, K, 1): RIGHT, (1, V, 0): RIGHT, (1, V, 1): RIGHT, (2, K, 0): RIGHT, (2, K, 1): RIGHT, (2, V, 0): RIGHT, (2, V, 1): RIGHT, (3, K, 0): LEFT, (3, K, 1): LEFT, (3, V, 0): LEFT, (3, V, 1): LEFT, (4, K, 0): UP, (4, K, 1): UP, (4, V, 0): UP, (4, V, 1): UP, (5, K, 0): UP, (5, K, 1): UP, (5, V, 0): RIGHT, (5, V, 1): UP, (6, K, 0): UP, (6, K, 1): UP, (6, V, 0): LEFT, (6, V, 1): LEFT, (7, K, 0): UP, (7, K, 1): UP, (7, V, 0): LEFT, (7, V, 1): LEFT, (8, K, 0): RELAY, (8, K, 1): RELAY, (8, V, 0): RELAY, (8, V, 1): RELAY}
+SENDS = (
+    (1, 3, 0, 1, 0, 2, -1),
+    (1, 4, 4, 1, 0, 2, 0),
+    (1, 3, 0, 1, 1, 2, -1),
+    (1, 4, 4, 1, 1, 2, 1),
+    (1, 3, 1, 2, 0, 0, 1),
+    (1, 3, 1, 2, 0, 1, 2),
+    (1, 4, 5, 2, 0, 2, 4),
+    (1, 3, 1, 2, 1, 2, 2),
+    (1, 4, 5, 2, 1, 2, 3),
+    (2, 1, 0, 3, 0, 2, -1),
+    (2, 7, 4, 3, 0, 2, 0),
+    (2, 1, 0, 3, 1, 2, -1),
+    (2, 7, 4, 3, 1, 2, 1),
+    (0, 0, 0, 4, 0, 2, -1),
+    (0, 0, 0, 4, 1, 2, -1),
+    (0, 0, 1, 5, 0, 1, 1),
+    (1, 3, 4, 5, 0, 0, 1),
+    (1, 4, 8, 5, 0, 0, 2),
+    (0, 0, 1, 5, 1, 2, 2),
+    (2, 1, 3, 6, 0, 2, 2),
+    (2, 7, 7, 6, 0, 2, 4),
+    (0, 0, 2, 6, 1, 2, 4),
+    (2, 1, 4, 7, 0, 0, 0),
+    (2, 1, 4, 7, 0, 1, 1),
+    (2, 7, 8, 7, 0, 2, 2),
+    (0, 0, 3, 7, 1, 2, 3),
+)
 ARRIVE = {(1, K): (2, 11), (1, V): (1, 6), (2, K): (4, 12), (2, V): (5, 4), (3, K): (3, 8), (3, V): (2, 9), (4, K): (1, 14), (4, V): (0, 3), (5, K): (3, 7), (5, V): (4, 13), (6, K): (6, 1), (6, V): (6, 2), (7, K): (4, 15), (7, V): (4, 10), (8, K): (4, 0), (8, V): (2, 5)}
-LEAVE = {(1, K, 0, 1): 1, (1, K, 1, 1): 1, (1, V, 0, 1): 0, (1, V, 1, 1): 0, (2, K, 0, 0): 2, (2, K, 0, 1): 3, (2, K, 1, 0): 2, (2, K, 1, 1): 3, (2, V, 0, 0): 1, (2, V, 0, 1): 4, (2, V, 1, 0): 1, (2, V, 1, 1): 4, (3, K, 0, 0): 1, (3, K, 1, 0): 1, (3, V, 0, 0): 0, (3, V, 1, 0): 0, (5, K, 0, 0): 2, (5, K, 1, 0): 2, (5, V, 0, 0): 1, (5, V, 0, 1): 2, (5, V, 1, 0): 1, (6, K, 0, 0): 4, (6, K, 1, 0): 4, (6, V, 0, 0): 4, (6, V, 0, 1): 2, (6, V, 1, 0): 4, (6, V, 1, 1): 2, (7, K, 0, 0): 3, (7, K, 1, 0): 3, (7, V, 0, 0): 2, (7, V, 0, 1): 0, (7, V, 1, 0): 2, (7, V, 1, 1): 0}
 RELAYED = {V: (0, 1), K: (3, 1)}
 RELAY_KEYS_AT = 1
 GROUPS = ((0,), (4,), (3, 1), (5, 8, 7), (2,), (6,))
@@ -80,14 +104,14 @@
     for load in loads:
         load.start()
 
-    def value_copy(src, dst, c, target):
+    def value_copy(src, dst, c, target, link=0, half=2):
         return pltpu.make_async_remote_copy(
-            wv.at[src, c, pl.ds(0, HEAD)], wv.at[dst, c, pl.ds(0, HEAD)], sv.at[dst, c], rv.at[dst, c],
+            wv.at[src, c, pl.ds(0, HEAD)], wv.at[dst, c, pl.ds(0, HEAD)], sv.at[link, dst, half], rv.at[dst, c],
             device_id={"ctx": target}, device_id_type=MESH)
 
-    def key_copy(src, dst, c, target):
+    def key_copy(src, dst, c, target, link=0, half=2):
         return pltpu.make_async_remote_copy(
-            wk.at[src, c], wk.at[dst, c], sk.at[dst, c], rk.at[dst, c],
+            wk.at[src, c], wk.at[dst, c], sk.at[link, dst, half], rk.at[dst, c],
             device_id={"ctx": target}, device_id_type=MESH)
 
     def doc_copy(d):
@@ -104,16 +128,16 @@
         buf = relay_v if kind == V else relay_k
         mine = wv.at[0, c, pl.ds(0, HEAD)] if kind == V else wk.at[0, c]
         return pltpu.make_async_remote_copy(
-            mine, buf.at[c], relay_sems.at[kind, 0, c], relay_sems.at[kind, 1, c],
+            mine, buf.at[c], relay_sems.at[kind, 0, 0], relay_sems.at[kind, 1, c],
             device_id={"ctx": relay}, device_id_type=MESH)
 
     def relayed_copy(kind, c):
         if kind == V:
             return pltpu.make_async_remote_copy(
-                relay_v.at[c], wv.at[8, c, pl.ds(0, HEAD)], relay_sems.at[kind, 2, c], rv.at[8, c],
+                relay_v.at[c], wv.at[8, c, pl.ds(0, HEAD)], relay_sems.at[kind, 2, 0], rv.at[8, c],
                 device_id={"ctx": down}, device_id_type=MESH)
         return pltpu.make_async_remote_copy(
-            relay_k.at[c], wk.at[8, c], relay_sems.at[kind, 2, c], rk.at[8, c],
+            relay_k.at[c], wk.at[8, c], relay_sems.at[kind, 2, 0], rk.at[8, c],
             device_id={"ctx": down}, device_id_type=MESH)
 
     def relay_own(kind, c):
@@ -133,66 +157,64 @@
                     relay_copy(kind, c).wait_recv()
                     relayed_copy(kind, c).start()
 
-    def drain_relays(c):
+    def drain_relays():
         for kind in RELAYED:
             @pl.when(me + 8 < count)
             def _():
-                relay_copy(kind, c).wait_send()
+                sent(kind, 8, relay_sems.at[kind, 0, 0])
 
             @pl.when(down >= 8)
             def _():
-                relayed_copy(kind, c).wait_send()
+                sent(kind, 8, relay_sems.at[kind, 2, 0])
 
     def copy_of(kind):
         return value_copy if kind == V else key_copy
 
-    def ways(d, kind, half):
-        link = ROUTE[d, kind, half]
-        if link == RELAY:
-            return []
-        plain, edge = SOURCES[link, d]
-        if link == UP:
-            return [(0, plain, up, me + 4 < count)]
-        special = x == 3 if link == RIGHT else x == 0
-        target = right if link == RIGHT else left
-        return [(0, plain, target, jnp.logical_not(special)), (1, edge, target, special)]
-
-    def send(way, d, kind, half, c):
-        _, src, target, there = way
-        if ROUTE[d, kind, 1 - half] != ROUTE[d, kind, half]:
-            if isinstance(c, int):
-                if c // 2 != half:
-                    return
-            else:
-                there = there & (c // 2 == half)
-        elif half:
+    targets = (up, right, left)
+    classes = (me >= 0, x == 0, x != 0, x < 3, x == 3, x == 1, x >= 2, x >= 1)
+
+    def open_to(entry):
+        link, who, src = entry[:3]
+        there = classes[who] & (src <= me)
+        return there & (me + 4 < count) if link == UP else there
+
+    def goes(entry, c):
+        half = entry[5]
+        return open_to(entry) if half == 2 else open_to(entry) & (c // 2 == half)
+
+    def sent(kind, d, sem, heads=pl.ds(0, KV_HEADS)):
+        ref = wv.at[d, heads, pl.ds(0, HEAD)] if kind == V else wk.at[d, heads]
+        pltpu.make_async_remote_copy(ref, ref, sem, sem, device_id={"ctx": up}, device_id_type=MESH).wait_send()
+
+    def send(entry, c):
+        link, _, src, d, kind, half, _ = entry
+        if isinstance(c, int) and half != 2 and c // 2 != half:
             return
-        when_sent(there & (src <= me), copy_of(kind)(src, d, c, target))
+        when_sent(goes(entry, c), copy_of(kind)(src, d, c, targets[link], link, half))
 
     def send_own(kind, c):
-        for d in (4, 1, 3):
-            for way in ways(d, kind, 0):
-                if way[1] == 0:
-                    send(way, d, kind, 0, c)
+        for entry in SENDS:
+            if entry[6] < 0 and entry[4] == kind:
+                send(entry, c)
 
     def stage_event(stage, c):
         first, after = [], {}
-        for (d, kind, half) in ROUTE:
-            for way in ways(d, kind, half):
-                if way[1] != 0 and LEAVE[d, kind, half, way[0]] == stage:
-                    if ARRIVE[way[1], kind][0] < stage:
-                        first.append((way, d, kind, half))
-                    else:
-                        after.setdefault((way[1], kind), []).append((way, d, kind, half))
+        for entry in SENDS:
+            _, _, src, _, kind, _, at = entry
+            if at == stage:
+                if ARRIVE[src, kind][0] < stage:
+                    first.append(entry)
+                else:
+                    after.setdefault((src, kind), []).append(entry)
         for entry in first:
-            send(*entry, c)
+            send(entry, c)
         relay_event(stage, 0, c)
         for d, kind in sorted((e for e in ARRIVE if ARRIVE[e][0] == stage), key=lambda e: ARRIVE[e][1]):
             @pl.when(d <= me)
             def _():
                 copy_of(kind)(d, d, c, up).wait_recv()
             for entry in after.get((d, kind), []):
-                send(*entry, c)
+                send(entry, c)
         relay_event(stage, 1, c)
 
     wv[:, :, HEAD:, :] = jnp.ones((ITEMS, KV_HEADS, VALUE_ROWS - HEAD, ROWS), jnp.bfloat16)
@@ -367,17 +389,13 @@
         def _():
             doc_copy(d).wait_send()
 
-    def drain(c, _):
-        for (d, kind, half) in ROUTE:
-            same = ROUTE[d, kind, 1 - half] == ROUTE[d, kind, half]
-            for way in ways(d, kind, half) if not (same and half) else []:
-                @pl.when(way[3] & (way[1] <= me) & ((c // 2 == half) | same))
-                def _():
-                    copy_of(kind)(d, d, c, up).wait_send()
-        drain_relays(c)
-        return 0
-
-    lax.fori_loop(0, KV_HEADS, drain, 0)
+    for entry in SENDS:
+        @pl.when(open_to(entry))
+        def _():
+            link, _, _, d, kind, half, _ = entry
+            sent(kind, d, (sv if kind == V else sk).at[link, d, half],
+                 pl.ds(0, KV_HEADS) if half == 2 else pl.ds(2 * half, 2))
+    drain_relays()
     for d in range(ITEMS):
         kept(wk, wk_hbm, wk_sem, d).wait()
         kept(wv, wv_hbm, wv_sem, d).wait()
@@ -501,7 +519,7 @@
             VMEM((8, 1, ROWS), jnp.int32),
             VMEM((HEAD // 2, ROWS), f32),
             VMEM((HEAD // 2, ROWS), f32),
-            dma(per_item), dma(per_item), dma(per_item), dma(per_item),
+            dma(per_item), dma(per_item), dma((3, ITEMS, 3)), dma((3, ITEMS, 3)),
             VMEM((KV_HEADS, HEAD, ROWS), bf), VMEM((KV_HEADS, ROWS, HEAD), bf), dma((2, 3, KV_HEADS)),
             dma((8,)), dma((8,)), dma((5,)), dma((HEADS // AT_ONCE,)), dma, dma((ITEMS,)), dma((ITEMS,)), dma((2,)),
         ],

time: 255 us -> 255 us (level)
  no operation moved by 1% of the time
where the time goes in v6:
time: 255 us; the launch traced here: 254 us
  Pallas kernels  254 us (100%)
    pallas_call x1, Pallas kernels, shards(): pl.pallas_call(finish, out_shape=jax.ShapeDtypeStruct((ROWS, HEADS * HEAD...  208 us
    pallas_call x1, Pallas kernels, shards(): pl.pallas_call(attend, out_shape=[jax.ShapeDtypeStruct((ROWS, HEADS * HEA...  46.1 us

profile of v6, /device:TPU:64, one launch (start us, length us, event | category | flops | bytes accessed | tf_op | source)
XLA Modules:
  0.0 254.4 jit_solution(3782638019046502883)
XLA Ops:
  0.0 46.1 %attend.1 = (bf16[256,4096]{1,0:T(8,128)(2,1)}, bf16[32,128,256]{2,1,0:T(8,128)(2,1)}, bf16[9,4,256,128]{3,2,1,0:T(8,128)(2,1)}, bf16[9,4,144,256]{3,2,1,0:T(8,1...) custom-call(s32[1,256]{1,0:T(1,128)} %bitcast.1, f32[1,128]{1,0:T(1,128)} %constant.2.clone.inverse_hbm, ...), custom_call_target="tpu_custom_call" | custom-call | flops 9663676416 | bytes 12582912 | tf_op jit(solution)/shard_map/attend/pallas_call | solution.py:493
  46.1 208.4 %finish.1 = bf16[256,4096]{1,0:T(8,128)(2,1)} custom-call(bf16[256,4096]{1,0:T(8,128)(2,1)} %get-tuple-element.11.found, f32[8,256]{1,0:T(8,128)} %get-tuple-element.12.start_hbm, f32[8,256]{1,0:T(8,128)} %get-tuple-element.13.bad_hbm, bf16[32,128,256]{2,1,0:T(8,128)(2,1)} %get-tuple-element.14.qt_hbm, bf16[9,4,256,128]{3,2,1,0:T(8,128)(2,1)} %get-tuple-element.15.wk_hbm, ...), custom_call_target="tpu_custom_call" | custom-call | flops 1048576 | bytes 16384 | tf_op jit(solution)/shard_map/finish/pallas_call | solution.py:530

commit v7 on v6

--- a/solution.py
+++ b/solution.py
@@ -29,8 +29,7 @@
     (1, 4, 4, 1, 0, 2, 0),
     (1, 3, 0, 1, 1, 2, -1),
     (1, 4, 4, 1, 1, 2, 1),
-    (1, 3, 1, 2, 0, 0, 1),
-    (1, 3, 1, 2, 0, 1, 2),
+    (1, 3, 1, 2, 0, 2, 1),
     (1, 4, 5, 2, 0, 2, 4),
     (1, 3, 1, 2, 1, 2, 2),
     (1, 4, 5, 2, 1, 2, 3),
@@ -47,8 +46,7 @@
     (2, 1, 3, 6, 0, 2, 2),
     (2, 7, 7, 6, 0, 2, 4),
     (0, 0, 2, 6, 1, 2, 4),
-    (2, 1, 4, 7, 0, 0, 0),
-    (2, 1, 4, 7, 0, 1, 1),
+    (2, 1, 4, 7, 0, 2, 0),
     (2, 7, 8, 7, 0, 2, 2),
     (0, 0, 3, 7, 1, 2, 3),
 )

time: 255 us -> 255 us (level)
  no operation moved by 1% of the time
where the time goes in v7:
time: 255 us; the launch traced here: 254 us
  Pallas kernels  254 us (100%)
    pallas_call x1, Pallas kernels, shards(): pl.pallas_call(finish, out_shape=jax.ShapeDtypeStruct((ROWS, HEADS * HEAD...  208 us
    pallas_call x1, Pallas kernels, shards(): pl.pallas_call(attend, out_shape=[jax.ShapeDtypeStruct((ROWS, HEADS * HEA...  46.1 us

profile of v7, /device:TPU:64, one launch (start us, length us, event | category | flops | bytes accessed | tf_op | source)
XLA Modules:
  0.0 254.4 jit_solution(15575599484827413267)
XLA Ops:
  0.0 46.1 %attend.1 = (bf16[256,4096]{1,0:T(8,128)(2,1)}, bf16[32,128,256]{2,1,0:T(8,128)(2,1)}, bf16[9,4,256,128]{3,2,1,0:T(8,128)(2,1)}, bf16[9,4,144,256]{3,2,1,0:T(8,1...) custom-call(s32[1,256]{1,0:T(1,128)} %bitcast.1, f32[1,128]{1,0:T(1,128)} %constant.2.clone.inverse_hbm, ...), custom_call_target="tpu_custom_call" | custom-call | flops 9663676416 | bytes 12582912 | tf_op jit(solution)/shard_map/attend/pallas_call | solution.py:491
  46.1 208.4 %finish.1 = bf16[256,4096]{1,0:T(8,128)(2,1)} custom-call(bf16[256,4096]{1,0:T(8,128)(2,1)} %get-tuple-element.11.found, f32[8,256]{1,0:T(8,128)} %get-tuple-element.12.start_hbm, f32[8,256]{1,0:T(8,128)} %get-tuple-element.13.bad_hbm, bf16[32,128,256]{2,1,0:T(8,128)(2,1)} %get-tuple-element.14.qt_hbm, bf16[9,4,256,128]{3,2,1,0:T(8,128)(2,1)} %get-tuple-element.15.wk_hbm, ...), custom_call_target="tpu_custom_call" | custom-call | flops 1048576 | bytes 16384 | tf_op jit(solution)/shard_map/finish/pallas_call | solution.py:528

commit v8 on v5

--- a/solution.py
+++ b/solution.py
@@ -184,6 +184,7 @@
                         first.append((way, d, kind, half))
                     else:
                         after.setdefault((way[1], kind), []).append((way, d, kind, half))
+        first.sort(key=lambda e: ROUTE[e[1:]] != UP)
         for entry in first:
             send(*entry, c)
         relay_event(stage, 0, c)
@@ -191,7 +192,7 @@
             @pl.when(d <= me)
             def _():
                 copy_of(kind)(d, d, c, up).wait_recv()
-            for entry in after.get((d, kind), []):
+            for entry in sorted(after.get((d, kind), []), key=lambda e: ROUTE[e[1:]] != UP):
                 send(*entry, c)
         relay_event(stage, 1, c)
 

time: 255 us -> 255 us (level)
  no operation moved by 1% of the time
where the time goes in v8:
time: 255 us; the launch traced here: 254 us
  Pallas kernels  254 us (100%)
    pallas_call x1, Pallas kernels, shards(): pl.pallas_call(finish, out_shape=jax.ShapeDtypeStruct((ROWS, HEADS * HEAD...  208 us
    pallas_call x1, Pallas kernels, shards(): pl.pallas_call(attend, out_shape=[jax.ShapeDtypeStruct((ROWS, HEADS * HEA...  45.3 us

profile of v8, /device:TPU:64, one launch (start us, length us, event | category | flops | bytes accessed | tf_op | source)
XLA Modules:
  0.0 253.6 jit_solution(17183800013988765952)
XLA Ops:
  0.0 45.3 %attend.1 = (bf16[256,4096]{1,0:T(8,128)(2,1)}, bf16[32,128,256]{2,1,0:T(8,128)(2,1)}, bf16[9,4,256,128]{3,2,1,0:T(8,128)(2,1)}, bf16[9,4,144,256]{3,2,1,0:T(8,1...) custom-call(s32[1,256]{1,0:T(1,128)} %bitcast.1, f32[1,128]{1,0:T(1,128)} %constant.2.clone.inverse_hbm, ...), custom_call_target="tpu_custom_call" | custom-call | flops 9663676416 | bytes 12582912 | tf_op jit(solution)/shard_map/attend/pallas_call | solution.py:476
  45.3 208.4 %finish.1 = bf16[256,4096]{1,0:T(8,128)(2,1)} custom-call(bf16[256,4096]{1,0:T(8,128)(2,1)} %get-tuple-element.11.found, f32[8,256]{1,0:T(8,128)} %get-tuple-element.12.start_hbm, f32[8,256]{1,0:T(8,128)} %get-tuple-element.13.bad_hbm, bf16[32,128,256]{2,1,0:T(8,128)(2,1)} %get-tuple-element.14.qt_hbm, bf16[9,4,256,128]{3,2,1,0:T(8,128)(2,1)} %get-tuple-element.15.wk_hbm, ...), custom_call_target="tpu_custom_call" | custom-call | flops 1048576 | bytes 16384 | tf_op jit(solution)/shard_map/finish/pallas_call | solution.py:513
